TPU v7x, 256 devices: a whole 4x4x8 slice. The times are simulated.
256 devices in a mesh: dp: 32 (over z, y_lo, core), chan: 8 (over y_hi, x).
Axes of the slice: x: 4, y: 4 (y_hi: 2, y_lo: 2; y = y_hi * 2 + y_lo), z: 8, core: 2. Of those that a mesh axis runs over, the one named last changes fastest.
Arguments:
- inputs: bfloat16 [1536, 196, 1024], P('dp', None, 'chan'), may hold values from -6 to 6
- norm_gain: float32 [1024], P('chan'), may hold values from 0.5 to 1.5
- norm_bias: float32 [1024], P('chan'), may hold values from -3 to 3
- w_first: bfloat16 [512, 196], replicated, may hold values from -0.4375 to 0.4375
- b_first: float32 [512], replicated, may hold values from -3 to 3
- w_second: bfloat16 [196, 512], replicated, may hold values from -0.25 to 0.25
- upstream: bfloat16 [1536, 196, 1024], P('dp', None, 'chan'), may hold values from -6 to 6
Outputs:
- grad_input: bfloat16 [1536, 196, 1024], P('dp', None, 'chan')
- grad_first: float32 [512, 196], P('dp')
- grad_second: float32 [196, 512], P(None, 'dp')
- grad_bias_first: float32 [512], P('dp')
- grad_gain: float32 [1024], P('chan')
- grad_shift: float32 [1024], P('chan')
All inputs are finite; a program needn't handle non-finite values.
Results may differ from a plain program's by a relative error of at most 0.0056.
Values sent between devices are 32-bit elements; how exact they have to be, the bound alone decides.
A program may use at most 64 MiB of HBM per device.

v0:
```python
import jax
import jax.numpy as jnp
from jax import lax
from jax.sharding import PartitionSpec as P

epsilon = 1e-06


def copy_for_each(value, axis):
    copies = jnp.broadcast_to(value, (lax.axis_size(axis), *value.shape))
    return lax.all_to_all(copies, axis, split_axis=0, concat_axis=0, tiled=True)


def taken_together(value, axis):
    everything = copy_for_each(value, axis)
    return jnp.sum(everything, axis=0)


def in_one(arrays, axis):
    ends = [0]
    for a in arrays:
        ends.append(ends[-1] + a.size)
    subtotal = taken_together(jnp.concatenate([a.ravel() for a in arrays]), axis)
    return tuple((subtotal[b:e].reshape(a.shape) for a, b, e in zip(arrays, ends, ends[1:])))


def split_up(value, dim, peers):
    dims = value.shape
    pieces = value.reshape(*dims[:dim], peers, dims[dim] // peers, *dims[dim + 1 :])
    return jnp.moveaxis(pieces, dim, 0)


def sum_at_owner(value, axis, dim):
    pieces = split_up(value, dim, lax.axis_size(axis))
    arrived = lax.all_to_all(pieces, axis, split_axis=0, concat_axis=0, tiled=True)
    return arrived.sum(axis=0)


def in_one_piece(arrays, axis, dim, along):
    columns = [a.reshape(*a.shape[:along], -1) for a in arrays]
    both = jnp.concatenate(columns, axis=along)
    out, at, gathered = (sum_at_owner(both, axis, dim), 0, [])
    for a, column in zip(arrays, columns):
        piece = out[..., at : at + column.shape[along]]
        gathered.append(piece.reshape(*piece.shape[:along], *a.shape[along:]))
        at += column.shape[along]
    return tuple(gathered)


def per_device(inputs, norm_gain, norm_bias, w_first, b_first, w_second, upstream):
    values = inputs.astype(jnp.float32)
    width = values.shape[2] * lax.axis_size("chan")
    images = values.shape[0] * lax.axis_size("dp")
    scale = 1.0 / images
    total, squares = in_one(
        (jnp.sum(values, axis=-1, keepdims=True), jnp.sum(values * values, axis=-1, keepdims=True)),
        "chan",
    )
    row_mean = total / width
    row_var = squares / width - row_mean * row_mean
    centered = values - row_mean
    inv_std = lax.rsqrt(row_var + epsilon)
    normed = centered * inv_std
    mixed_in = (normed * norm_gain + norm_bias).astype(jnp.bfloat16)
    pre_act = (
        jnp.einsum("kp,bpc->bkc", w_first, mixed_in, preferred_element_type=jnp.float32)
        + b_first[None, :, None]
    )
    gauss_cdf = 0.5 * (1.0 + lax.erf(pre_act * 0.7071067811865476))
    gauss_pdf = jnp.exp(-0.5 * pre_act * pre_act) * 0.3989422804014327
    activated = (pre_act * gauss_cdf).astype(jnp.bfloat16)
    grad_act = jnp.einsum("pk,bpc->bkc", w_second, upstream, preferred_element_type=jnp.float32)
    grad_pre = (grad_act * (gauss_cdf + pre_act * gauss_pdf)).astype(jnp.bfloat16)
    second_t = (
        jnp.einsum("bkc,bpc->kp", activated, upstream, preferred_element_type=jnp.float32) * scale
    )
    first_w = (
        jnp.einsum("bkc,bpc->kp", grad_pre, mixed_in, preferred_element_type=jnp.float32) * scale
    )
    first_b = jnp.sum(grad_pre.astype(jnp.float32), axis=(0, 2)) * scale
    grad_mixed = jnp.einsum("kp,bkc->bpc", w_first, grad_pre, preferred_element_type=jnp.float32)
    grad_normed = grad_mixed * norm_gain
    first_sum, second_sum = in_one(
        (
            jnp.sum(grad_normed, axis=-1, keepdims=True),
            jnp.sum(grad_normed * normed, axis=-1, keepdims=True),
        ),
        "chan",
    )
    grad_input = (
        upstream.astype(jnp.float32)
        + inv_std * (grad_normed - first_sum / width - normed * second_sum / width)
    ).astype(jnp.bfloat16)
    grad_gain, grad_shift = in_one(
        (
            jnp.sum(grad_mixed * normed, axis=(0, 1)) * scale,
            jnp.sum(grad_mixed, axis=(0, 1)) * scale,
        ),
        "dp",
    )
    shard_w, shard_t, shard_b = in_one_piece((first_w, second_t, first_b), "dp", 0, 1)
    owned_w, owned_t, owned_b = in_one((shard_w, shard_t, shard_b), "chan")
    return (grad_input, owned_w, owned_t.T, owned_b, grad_gain, grad_shift)


def solution(mesh):
    in_specs = (P("dp", None, "chan"), P("chan"), P("chan"), P(), P(), P(), P("dp", None, "chan"))
    out_specs = (P("dp", None, "chan"), P("dp", None), P(None, "dp"), P("dp"), P("chan"), P("chan"))
    return jax.shard_map(
        per_device, mesh=mesh, in_specs=in_specs, out_specs=out_specs, check_vma=False
    )
```

profile of v0, /device:TPU:2, one launch (start us, length us, event | category | flops | bytes accessed | tf_op | source)
XLA Modules:
  0.0 143.9 jit_solution(7652559280606895878)
XLA Ops:
  0.7 5.2 %convert_reduce_fusion.1 = (f32[48,196]{1,0:T(8,128)S(1)}, f32[48,196]{1,0:T(8,128)S(1)}) fusion(bf16[48,196,128]{2,0,1:T(8,128)(2,1)} %param.7), kind=kLoop, calls=%fused_computation.16 | loop fusion | flops 4798080 | bytes 2483712 | tf_op jit(solution)/shard_map/reduce_sum | solution.py:56
  5.8 0.1 reshape_broadcast_in_dim.12
  6.0 0.1 reshape_broadcast_in_dim.13
  6.2 0.3 broadcast_in_dim.16
  6.5 18.6 %all_to_all.29 = f32[8,1,18816]{2,1,0:T(1,128)S(1)} all-to-all(f32[8,1,18816]{2,1,0:T(1,128)S(1)} %broadcast_in_dim.16), channel_id=1, replica_groups=mesh['dp'=32,'chan'=8] {'chan'}, dimensions={0} | all-to-all | bytes 1204224 | tf_op jit(solution)/shard_map/all_to_all | solution.py:11
  25.1 0.4 reduce_sum.110
  25.5 0.1 slice_multiply_fusion.2
  25.6 0.1 div.22
  25.7 0.1 div.24
  26.0 4.3 %fusion.33 = f32[48,128,512]{2,1,0:T(8,128)S(1)} fusion(f32[128]{0:T(128)S(1)} %copy-done.8, f32[128]{0:T(128)S(1)} %copy-done.7, f32[48,196]{1,0:T(8,128)S(1)} %div.24, f32[48,196]{1,0:T(8,128)S(1)} %add_rsqrt_fusion, bf16[48,196,128]{2,0,1:T(8,128)(2,1)S(1)} %copy-done.2, bf16[512,196]{0,1:T(8,128)(2,1)S(1)} %copy-done), kind=kOutput, calls=%fused_computation.39 | convolution fusion | flops 1240350720 | bytes 15268352 | tf_op jit(solution)/shard_map/kp,bpc->bkc/dot_general | solution.py:66
  30.3 3.1 %fusion.46 = f32[512,196]{0,1:T(8,128)S(1)} fusion(bf16[48,196,128]{2,0,1:T(8,128)(2,1)S(1)} %copy-done.4, f32[48,128,512]{2,1,0:T(8,128)S(1)} %fusion.33, f32[512]{0:T(512)S(1)} %copy-done.10), kind=kOutput, calls=%fused_computation.43 | convolution fusion | flops 1252100096 | bytes 15394816 | tf_op jit(solution)/shard_map/bkc,bpc->kp/dot_general | solution.py:75
  33.4 7.8 %convert_reduce_fusion = (f32[512]{0:T(512)S(1)}, bf16[48,512,128]{1,2,0:T(8,128)(2,1)S(1)}) fusion(f32[48,128,512]{2,1,0:T(8,128)S(1)} %fusion.33, f32[512]{0:T(512)S(1)} %copy-done.10, bf16[196,512]{1,0:T(8,128)(2,1)S(1)} %copy-done.9, bf16[48,196,128]{2,0,1:T(8,128)(2,1)S(1)} %copy-done.4), kind=kOutput, calls=%fused_computation.13 | convolution fusion | flops 1274019328 | bytes 21487616 | tf_op jit(solution)/shard_map/pk,bpc->bkc/dot_general | solution.py:72
  41.1 2.3 %fusion.61 = (f32[128]{0:T(128)S(1)}, f32[48,128,196]{1,2,0:T(8,128)S(1)}) fusion(bf16[48,512,128]{1,2,0:T(8,128)(2,1)S(1)} %get-tuple-element.60, bf16[512,196]{0,1:T(8,128)(2,1)S(1)} %copy-done), kind=kOutput, calls=%fused_computation.65 | convolution fusion | flops 1234329472 | bytes 11309568 | tf_op jit(solution)/shard_map/kp,bkc->bpc/dot_general | solution.py:81
  43.4 0.4 copy-done.3
  43.8 2.3 %copy-done.1 = f32[48,128,196]{1,2,0:T(8,128)} copy-done((f32[48,128,196]{1,2,0:T(8,128)}, f32[48,128,196]{1,2,0:T(8,128)S(1)}, u32[]{:S(2)}) %copy-start.1) | copy-done | bytes 4816920
  46.1 6.9 %fusion.27 = (f32[128]{0:T(128)S(1)}, f32[48,196]{1,0:T(8,128)S(1)}, f32[48,196]{1,0:T(8,128)S(1)}) fusion(f32[48,128,196]{1,2,0:T(8,128)S(1)} %get-tuple-element.58, f32[48,196]{1,0:T(8,128)S(1)} %div.24, f32[48,196]{1,0:T(8,128)S(1)} %add_rsqrt_fusion, bf16[48,196,128]{2,0,1:T(8,128)(2,1)S(1)} %copy-done.2, f32[128]{0:T(128)S(1)} %copy-done.7), kind=kLoop, calls=%fused_computation.33 | loop fusion | flops 10819072 | bytes 7376896 | tf_op jit(solution)/shard_map/reduce_sum | solution.py:96
  53.1 0.6 broadcast_in_dim.19
  53.7 9.3 %all-to-all-start.4 = ((f32[32,1,256]{2,1,0:T(1,128)}), f32[32,1,256]{2,1,0:T(1,128)}, u32[]{:S(2)}, u32[]{:S(2)}) async-start(f32[32,1,256]{2,1,0:T(1,128)} %broadcast_in_dim.19), calls=%async_computation.4 | async-start | bytes 65536 | tf_op jit(solution)/shard_map/all_to_all | solution.py:11
  63.0 0.1 reshape_broadcast_in_dim.15
  63.2 0.1 reshape_broadcast_in_dim.14
  63.4 1.0 copy.77
  64.4 0.2 mul.152
  64.6 6.3 %all-to-all-done.4 = f32[32,1,256]{2,1,0:T(1,128)} async-done(((f32[32,1,256]{2,1,0:T(1,128)}), f32[32,1,256]{2,1,0:T(1,128)}, u32[]{:S(2)}, u32[]{:S(2)}) %all-to-all-start.4) | async-done | bytes 32800 | tf_op jit(solution)/shard_map/all_to_all | solution.py:11
  70.9 1.1 broadcast_in_dim.17
  72.0 4.6 %all-to-all-start.1 = ((f32[8,1,18816]{2,1,0:T(1,128)}), f32[8,1,18816]{2,1,0:T(1,128)S(1)}, u32[]{:S(2)}, u32[]{:S(2)}) async-start(f32[8,1,18816]{2,1,0:T(1,128)} %broadcast_in_dim.17), calls=%async_computation.1 | async-start | bytes 1204224 | tf_op jit(solution)/shard_map/all_to_all | solution.py:11
  76.7 6.8 %fusion.38 = f32[512,196]{0,1:T(8,128)} fusion(bf16[48,512,128]{1,2,0:T(8,128)(2,1)} %copy-done.3, f32[128]{0:T(128)S(1)} %copy-done.8, f32[128]{0:T(128)S(1)} %copy-done.7, f32[48,196]{1,0:T(8,128)S(1)} %div.24, f32[48,196]{1,0:T(8,128)} %copy-done.5, bf16[48,196,128]{2,0,1:T(8,128)(2,1)S(1)} %copy-done.2), kind=kOutput, calls=%fused_computation.41 | convolution fusion | flops 1240451072 | bytes 9177600 | tf_op jit(solution)/shard_map/bkc,bpc->kp/dot_general | solution.py:78
  83.4 2.0 %copy.74 = f32[512,196]{1,0:T(8,128)} copy(f32[512,196]{0,1:T(8,128)} %fusion.38) | data formatting | bytes 802816 | tf_op jit(solution)/shard_map/mul | solution.py:78
  85.4 2.5 %pad_maximum_fusion = f32[32,16,393]{2,1,0:T(8,128)} fusion(f32[32,16,1]{2,1,0:T(8,128)S(1)} %mul.152, f32[32,16,196]{2,1,0:T(8,128)} %bitcast.58, f32[32,16,196]{2,1,0:T(8,128)} %bitcast.59), kind=kLoop, calls=%fused_computation.44 | loop fusion | flops 402432 | bytes 1609728 | tf_op jit(solution)/shard_map/concatenate | solution.py:41
  87.9 0.6 all-to-all-done.1
  88.6 4.7 %all-to-all-start.2 = ((f32[32,16,393]{2,1,0:T(8,128)}), f32[32,16,393]{2,1,0:T(8,128)}, u32[]{:S(2)}, u32[]{:S(2)}) async-start(f32[32,16,393]{2,1,0:T(8,128)} %pad_maximum_fusion), calls=%async_computation.2 | async-start | bytes 2097152 | tf_op jit(solution)/shard_map/all_to_all | solution.py:35
  93.3 0.8 reduce_sum.119
  94.1 0.5 fusion.60
  94.6 0.4 reduce_sum.113
  95.1 0.1 div.26
  95.3 0.1 mul.139
  95.4 27.0 %all-to-all-done.2 = f32[32,16,393]{2,1,0:T(8,128)} async-done(((f32[32,16,393]{2,1,0:T(8,128)}), f32[32,16,393]{2,1,0:T(8,128)}, u32[]{:S(2)}, u32[]{:S(2)}) %all-to-all-start.2) | async-done | bytes 804896 | tf_op jit(solution)/shard_map/all_to_all | solution.py:35
  122.4 1.3 reduce_sum.115
  123.7 0.2 slice_reduce_fusion
  124.0 0.1 reshape.142
  124.1 0.1 reshape.141
  124.3 0.8 broadcast_in_dim.18
  125.1 6.7 %all-to-all-start.3 = ((f32[8,1,6288]{2,1,0:T(1,128)}), f32[8,1,6288]{2,1,0:T(1,128)S(1)}, u32[]{:S(2)}, u32[]{:S(2)}) async-start(f32[8,1,6288]{2,1,0:T(1,128)} %broadcast_in_dim.18), calls=%async_computation.3 | async-start | bytes 409600 | tf_op jit(solution)/shard_map/all_to_all | solution.py:11
  131.8 8.2 %fusion.26 = bf16[48,196,128]{2,1,0:T(8,128)(2,1)S(1)} fusion(f32[48,128,196]{1,2,0:T(8,128)} %copy-done.1, f32[48,196]{1,0:T(8,128)S(1)} %mul.139, f32[48,196]{1,0:T(8,128)S(1)} %div.26, f32[128]{0:T(128)S(1)} %copy-done.7, f32[48,196]{1,0:T(8,128)S(1)} %div.24, f32[48,196]{1,0:T(8,128)S(1)} %copy-done.6, bf16[48,196,128]{2,0,1:T(8,128)(2,1)} %param.13, ...), kind=kLoop, calls=%fused_computation.32 | loop fusion | flops 14450688 | bytes 12193280 | tf_op jit(solution)/shard_map/convert_element_type | solution.py:93
  140.0 1.7 %copy.81 = bf16[48,196,128]{2,0,1:T(8,128)(2,1)} copy(bf16[48,196,128]{2,1,0:T(8,128)(2,1)S(1)} %fusion.26) | data formatting | bytes 4816896
  141.7 0.2 reduce_sum.116
  141.9 0.5 slice.91
  142.5 0.7 reshape.145
  143.2 0.7 reshape.144
  (31 shorter events, 0.6 us)
Async XLA Ops:
  0.6 25.3 %copy-start = (bf16[512,196]{0,1:T(8,128)(2,1)S(1)}, bf16[512,196]{0,1:T(8,128)(2,1)}, u32[]{:S(2)}) copy-start(bf16[512,196]{0,1:T(8,128)(2,1)} %param.10) | copy-start | bytes 602116
  0.6 25.3 %copy-start.2 = (bf16[48,196,128]{2,0,1:T(8,128)(2,1)S(1)}, bf16[48,196,128]{2,0,1:T(8,128)(2,1)}, u32[]{:S(2)}) copy-start(bf16[48,196,128]{2,0,1:T(8,128)(2,1)} %param.7) | copy-start | bytes 7225348
  0.7 25.3 %copy-start.7 = (f32[128]{0:T(128)S(1)}, f32[128]{0:T(128)}, u32[]{:S(2)}) copy-start(f32[128]{0:T(128)} %param.8) | copy-start | bytes 1540
  0.7 25.3 %copy-start.8 = (f32[128]{0:T(128)S(1)}, f32[128]{0:T(128)}, u32[]{:S(2)}) copy-start(f32[128]{0:T(128)} %param.9) | copy-start | bytes 1540
  25.9 17.9 %copy-start.5 = (f32[48,196]{1,0:T(8,128)}, f32[48,196]{1,0:T(8,128)S(1)}, u32[]{:S(2)}) copy-start(f32[48,196]{1,0:T(8,128)S(1)} %add_rsqrt_fusion) | copy-start | bytes 112900
  25.9 4.3 %copy-start.4 = (bf16[48,196,128]{2,0,1:T(8,128)(2,1)S(1)}, bf16[48,196,128]{2,0,1:T(8,128)(2,1)}, u32[]{:S(2)}) copy-start(bf16[48,196,128]{2,0,1:T(8,128)(2,1)} %param.13) | copy-start | bytes 7225348
  26.0 4.3 %copy-start.10 = (f32[512]{0:T(512)S(1)}, f32[512]{0:T(512)}, u32[]{:S(2)}) copy-start(f32[512]{0:T(512)} %param.11) | copy-start | bytes 6148
  30.3 3.1 %copy-start.9 = (bf16[196,512]{1,0:T(8,128)(2,1)S(1)}, bf16[196,512]{1,0:T(8,128)(2,1)}, u32[]{:S(2)}) copy-start(bf16[196,512]{1,0:T(8,128)(2,1)} %param.12) | copy-start | bytes 602116
  41.1 2.7 %copy-start.3 = (bf16[48,512,128]{1,2,0:T(8,128)(2,1)}, bf16[48,512,128]{1,2,0:T(8,128)(2,1)S(1)}, u32[]{:S(2)}) copy-start(bf16[48,512,128]{1,2,0:T(8,128)(2,1)S(1)} %get-tuple-element.60) | copy-start | bytes 18874372
  43.8 2.3 %copy-start.1 = (f32[48,128,196]{1,2,0:T(8,128)}, f32[48,128,196]{1,2,0:T(8,128)S(1)}, u32[]{:S(2)}) copy-start(f32[48,128,196]{1,2,0:T(8,128)S(1)} %get-tuple-element.58) | copy-start | bytes 14450692
  53.7 17.2 %all-to-all-start.4 = ((f32[32,1,256]{2,1,0:T(1,128)}), f32[32,1,256]{2,1,0:T(1,128)}, u32[]{:S(2)}, u32[]{:S(2)}) async-start(f32[32,1,256]{2,1,0:T(1,128)} %broadcast_in_dim.19), calls=%async_computation.4 | async-start | bytes 65536 | tf_op jit(solution)/shard_map/all_to_all | solution.py:11
  72.0 16.5 %all-to-all-start.1 = ((f32[8,1,18816]{2,1,0:T(1,128)}), f32[8,1,18816]{2,1,0:T(1,128)S(1)}, u32[]{:S(2)}, u32[]{:S(2)}) async-start(f32[8,1,18816]{2,1,0:T(1,128)} %broadcast_in_dim.17), calls=%async_computation.1 | async-start | bytes 1204224 | tf_op jit(solution)/shard_map/all_to_all | solution.py:11
  87.9 43.9 %copy-start.6 = (f32[48,196]{1,0:T(8,128)S(1)}, f32[48,196]{1,0:T(8,128)}, u32[]{:S(2)}) copy-start(f32[48,196]{1,0:T(8,128)} %copy-done.5) | copy-start | bytes 112900
  88.6 33.9 %all-to-all-start.2 = ((f32[32,16,393]{2,1,0:T(8,128)}), f32[32,16,393]{2,1,0:T(8,128)}, u32[]{:S(2)}, u32[]{:S(2)}) async-start(f32[32,16,393]{2,1,0:T(8,128)} %pad_maximum_fusion), calls=%async_computation.2 | async-start | bytes 2097152 | tf_op jit(solution)/shard_map/all_to_all | solution.py:35
  125.1 16.6 %all-to-all-start.3 = ((f32[8,1,6288]{2,1,0:T(1,128)}), f32[8,1,6288]{2,1,0:T(1,128)S(1)}, u32[]{:S(2)}, u32[]{:S(2)}) async-start(f32[8,1,6288]{2,1,0:T(1,128)} %broadcast_in_dim.18), calls=%async_computation.3 | async-start | bytes 409600 | tf_op jit(solution)/shard_map/all_to_all | solution.py:11
where the time goes:
time: 145 us; the launch traced here: 144 us
  waiting for transfers between devices  34 us (23%)
  other arithmetic  26.3 us (18%)
  starting transfers between devices  25.4 us (18%)
  matrix products  24.1 us (17%)
  blocking collectives  18.6 us (13%)
  local copies, waits for them, and re-layouts  14.6 us (10%)
    all_to_all x1, waiting for transfers between devices, sum_at_owner(): lax.all_to_all(pieces, axis, split_axis=0, concat_axis=0, tiled=True)  27 us
    all_to_all x3, starting transfers between devices, copy_for_each(): return lax.all_to_all(copies, axis, split_axis=0, concat_axis=0, tiled=True)  20.7 us
    all_to_all x1, blocking collectives, copy_for_each(): return lax.all_to_all(copies, axis, split_axis=0, concat_axis=0, tiled=True)  18.6 us
    convert_element_type x1, other arithmetic, per_device(): grad_input = (upstream.astype(jnp.float32) + inv_std * (grad_normed - fir...  8.16 us
    dot_general x1, matrix products, per_device(): jnp.einsum('pk,bpc->bkc', w_second, upstream, preferred_element_type=jnp....  7.76 us
    all_to_all x3, waiting for transfers between devices, copy_for_each(): return lax.all_to_all(copies, axis, split_axis=0, concat_axis=0, tiled=True)  6.95 us
    reduce_sum x1, other arithmetic, per_device(): jnp.sum(grad_mixed * normed, axis=(0, 1)) * scale  6.94 us
    dot_general x1, matrix products, per_device(): jnp.einsum('bkc,bpc->kp', grad_pre, mixed_in, preferred_element_type=jnp....  6.75 us
  transfers between devices with their start and end apart: 4, of which 3 were waited for; matrix products, arithmetic and copies ran while one was open for 17% of the time, Pallas kernels for 0%

commit v1 on v0

v1 whole, which is shorter than its diff:
```python
import functools

import jax
import jax.numpy as jnp
from jax import lax
from jax.experimental import pallas as pl
from jax.experimental.pallas import tpu as pltpu
from jax.sharding import PartitionSpec as P

EPS = 1e-06
NB = 16
PP = 208
LANES = 128
F32 = jnp.float32
BF16 = jnp.bfloat16


def contract_lanes(a, b):
    return lax.dot_general(a, b, (((1,), (1,)), ((), ())), preferred_element_type=F32)


def kernel(
    n_dp, n_chan, patches, width, scale,
    x_hbm, u_hbm, gain_ref, bias_ref, w1a_ref, w1t_ref, w2t_ref,
    out_ref, first_ref, second_ref, vec_ref,
    x_v, u_v, mx, up, ga, gp, act, normed_n, gm_n, tmp, inv_d, acc,
    a_send, a_recv, b_send, b_recv, p0_recv, csum, c1_recv, c1_sum, c2_recv, d_send, d_recv,
    load_sem, as_sem, ar_sem, bs_sem, br_sem, p0s_sem, p0r_sem, c1s_sem, c1r_sem, c2s_sem, c2r_sem, ds_sem, dr_sem,
):
    me_d = lax.axis_index("dp")
    me_c = lax.axis_index("chan")
    core = lax.rem(me_d, 2)
    me_g = lax.div(me_d, 2)
    groups = n_dp // 2
    chunks = x_v.shape[1] // NB
    hid = w1a_ref.shape[0]
    half = hid // 2
    tiles = NB // 2
    span = NB * LANES

    def chan_peer(j):
        return lax.rem(me_c + j, n_chan)

    def dp_peer(j):
        return lax.rem(me_d + j, n_dp)

    def remote(src, dst, ssem, rsem, dp, chan):
        return pltpu.make_async_remote_copy(
            src_ref=src, dst_ref=dst, send_sem=ssem, recv_sem=rsem,
            device_id={"dp": dp, "chan": chan}, device_id_type=pl.DeviceIdType.MESH,
        )

    barrier = pltpu.get_barrier_semaphore()
    for j in range(1, n_chan):
        pl.semaphore_signal(barrier, inc=1, device_id={"dp": me_d, "chan": chan_peer(j)}, device_id_type=pl.DeviceIdType.MESH)
    for j in range(1, n_dp):
        pl.semaphore_signal(barrier, inc=1, device_id={"dp": dp_peer(j), "chan": me_c}, device_id_type=pl.DeviceIdType.MESH)

    def load(which, src, dst, ch):
        rows = pl.ds(ch * NB, NB)
        return pltpu.make_async_copy(src.at[:, rows, :], dst.at[:, rows, :], load_sem.at[which, ch])

    for ch in range(chunks):
        load(0, x_hbm, x_v, ch).start()
    for ch in range(chunks):
        load(1, u_hbm, u_v, ch).start()

    lane = lax.broadcasted_iota(jnp.int32, (NB, LANES), 1)

    def lane_tiles(body, init):
        out = []
        for lo in range(0, patches, LANES):
            count = min(LANES, patches - lo)

            def step(q, carry, lo=lo):
                for i in range(4):
                    carry = body(lo + q * 4 + i, q * 4 + i, carry)
                return carry

            out.append(lax.fori_loop(0, count // 4, step, init))
        return out

    zero = jnp.zeros((NB, LANES), F32)

    for ch in range(chunks):
        load(0, x_hbm, x_v, ch).wait()

        def stat(p, at, carry, ch=ch):
            s, q = carry
            v = x_v[p, pl.ds(ch * NB, NB), :].astype(F32)
            hit = lane == at
            s = jnp.where(hit, jnp.sum(v, axis=-1, keepdims=True), s)
            q = jnp.where(hit, jnp.sum(v * v, axis=-1, keepdims=True), q)
            return s, q

        for t, (s, q) in enumerate(lane_tiles(stat, (zero, zero))):
            a_send[ch, :, pl.ds(t * LANES, LANES)] = s
            a_send[ch, :, pl.ds((2 + t) * LANES, LANES)] = q
        if ch == 0:
            pl.semaphore_wait(barrier, n_chan - 1 + n_dp - 1)
        for j in range(1, n_chan):
            remote(a_send.at[ch], a_recv.at[ch, j], as_sem.at[ch, j], ar_sem.at[ch, j], me_d, chan_peer(j)).start()

    def regroup(g, ch, dst, value, fill):
        for i in range(16):
            tmp[pl.ds(i * NB, NB), :] = value(i)
        for b in range(NB):
            v = tmp[pl.ds(b, 16, stride=NB), :]
            if fill is not None:
                v = fill(v)
            at = pl.multiple_of(ch * span + b * LANES, LANES)
            rows = pl.ds(pl.multiple_of(g * 16, 16), 16)
            dst[rows, pl.ds(at, LANES)] = v.astype(BF16)

    full = patches // 16
    rest = patches - full * 16
    sub = lax.broadcasted_iota(jnp.int32, (16, LANES), 0)

    for ch in range(chunks):
        load(1, u_hbm, u_v, ch).wait()

        def up_group(g, _, ch=ch):
            regroup(g, ch, up, lambda i: u_v[g * 16 + i, pl.ds(ch * NB, NB), :].astype(F32), None)
            return 0

        lax.fori_loop(0, full, up_group, 0)
        regroup(
            full, ch, up,
            lambda i, ch=ch: u_v[full * 16 + min(i, rest - 1), pl.ds(ch * NB, NB), :].astype(F32),
            lambda v: jnp.where(sub < rest, v, 0.0),
        )

    def ga_tile(n, _):
        at = pl.ds(pl.multiple_of(n * 256, 256), 256)
        ga[:, at] = jnp.dot(w2t_ref[...], up[:, at], preferred_element_type=F32)
        return 0

    lax.fori_loop(0, chunks * tiles, ga_tile, 0)

    gain = gain_ref[...]
    bias = bias_ref[...]

    def wait_a(ch):
        total = a_send[ch]
        for j in range(1, n_chan):
            remote(a_send.at[ch], a_recv.at[ch, j], as_sem.at[ch, j], ar_sem.at[ch, j], me_d, chan_peer(j)).wait_recv()
            total = total + a_recv[ch, j]
        mean = total[:, : 2 * LANES] / width
        var = total[:, 2 * LANES :] / width - mean * mean
        return mean, lax.rsqrt(var + EPS)

    def column(value, i):
        return jnp.broadcast_to(value[:, i : i + 1], (NB, LANES))

    def normalise(ch):
        mean, inv = wait_a(ch)
        inv_d[ch] = inv
        mean_ref, inv_ref = a_send.at[ch], inv_d.at[ch]

        def one(g, mean16, inv16, count):
            def value(i):
                i = min(i, count - 1)
                p = g * 16 + i
                v = x_v[p, pl.ds(ch * NB, NB), :].astype(F32)
                normed = (v - column(mean16, i)) * column(inv16, i)
                normed_n[ch, pl.ds(pl.multiple_of(p * NB, NB), NB), :] = normed
                return normed * gain + bias

            fill = None
            if count < 16:
                fill = lambda v: jnp.where(sub < rest, v, jnp.where(sub < rest + 3, 1.0, 0.0))
            regroup(g, ch, mx, value, fill)

        for t in range(2):
            m_t = mean[:, t * LANES : (t + 1) * LANES]
            i_t = inv[:, t * LANES : (t + 1) * LANES]
            per = LANES // 16

            def group(g, carry, t=t):
                m, v = carry
                one(t * per + g, m, v, 16)
                return pltpu.roll(m, LANES - 16, 1), pltpu.roll(v, LANES - 16, 1)

            m_t, i_t = lax.fori_loop(0, min(per, full - t * per), group, (m_t, i_t))
        one(full, m_t, i_t, rest)

    def hidden(h, ch):
        rows = pl.ds(h * half, half)

        def tile(n, _):
            at = pl.ds(pl.multiple_of(ch * span + n * 256, 256), 256)
            pre = jnp.dot(w1a_ref[rows, :], mx[:, at], preferred_element_type=F32)
            t = pre * 0.7071067811865476
            cdf = 0.5 * lax.erf(t) + 0.5
            act[:, pl.ds(pl.multiple_of(n * 256, 256), 256)] = (pre * cdf).astype(BF16)
            slope = cdf + (t * 0.5641895835477563) * jnp.exp(-(t * t))
            gp[rows, at] = (ga[rows, at] * slope).astype(BF16)
            return 0

        lax.fori_loop(0, tiles, tile, 0)
        at = pl.ds(ch * span, span)
        first = contract_lanes(gp[rows, at], mx[:, at]).reshape(groups, 2, -1, PP)
        second = contract_lanes(act[...], up[:, at]).reshape(groups, 2, -1, PP)
        if ch:
            first = first + acc[h, :, :, :, pl.ds(0, PP)]
            second = second + acc[h, :, :, :, pl.ds(256, PP)]
        acc[h, :, :, :, pl.ds(0, PP)] = first
        acc[h, :, :, :, pl.ds(256, PP)] = second

    def p0(h):
        return remote(acc.at[h, :, 1 - core], p0_recv.at[h], p0s_sem.at[h], p0r_sem.at[h], me_d + 1 - 2 * core, me_c)

    def c1(h, j):
        g = lax.rem(me_g + j, groups)
        return remote(csum.at[h, g], c1_recv.at[h, me_g], c1s_sem.at[h, j], c1r_sem.at[h, me_g], 2 * g + core, me_c)

    def c1_arrival(h, j):
        g = lax.rem(me_g + j, groups)
        return remote(csum.at[h, g], c1_recv.at[h, g], c1s_sem.at[h, j], c1r_sem.at[h, g], 2 * g + core, me_c)

    def c2(h, j):
        return remote(c1_sum.at[h], c2_recv.at[h, me_c], c2s_sem.at[h, j], c2r_sem.at[h, me_c], me_d, chan_peer(j))

    def c2_arrival(h, j):
        c = chan_peer(j)
        return remote(c1_sum.at[h], c2_recv.at[h, c], c2s_sem.at[h, j], c2r_sem.at[h, c], me_d, c)

    def pair_done(h):
        p0(h).wait()
        csum[h] = acc[h, :, core] + p0_recv[h]
        for j in range(1, groups):
            c1(h, j).start()

    def group_done(h):
        c1_recv[h, me_g] = csum[h, me_g]
        for j in range(1, groups):
            c1_arrival(h, j).wait_recv()
        total = c1_recv[h, 0]
        for g in range(1, groups):
            total = total + c1_recv[h, g]
        c1_sum[h] = total
        c2_recv[h, me_c] = total
        for j in range(1, n_chan):
            c2(h, j).start()

    def all_done(h):
        for j in range(1, n_chan):
            c2_arrival(h, j).wait_recv()
        total = c2_recv[h, 0]
        for c in range(1, n_chan):
            total = total + c2_recv[h, c]
        total = total * scale
        first_ref[pl.ds(h * 8, 8), :] = total[:, :256]
        second_ref[pl.ds(h * 8, 8), :] = total[:, 256 : 256 + patches]

    for ch in range(chunks):
        normalise(ch)
        hidden(0, ch)
    p0(0).start()
    for ch in range(chunks):
        hidden(1, ch)
        if ch == 0:
            pair_done(0)
    p0(1).start()

    grads = (zero, zero)
    for ch in range(chunks):

        def back(n, _, ch=ch):
            at = pl.ds(pl.multiple_of(ch * span + n * 256, 256), 256)
            gm = jnp.dot(w1t_ref[...], gp[:, at], preferred_element_type=F32)
            for i in range(2):
                gm_n[ch, pl.ds(n * 2 + i, patches, stride=NB), :] = gm[:, i * LANES : (i + 1) * LANES]
            return 0

        lax.fori_loop(0, tiles, back, 0)

        def sums(p, at, carry, ch=ch):
            f, s, dg, ds = carry
            rows = pl.ds(pl.multiple_of(p * NB, NB), NB)
            gm = gm_n[ch, rows, :]
            normed = normed_n[ch, rows, :]
            both = gm * normed
            hit = lane == at
            f = jnp.where(hit, jnp.sum(gm * gain, axis=-1, keepdims=True), f)
            s = jnp.where(hit, jnp.sum(both * gain, axis=-1, keepdims=True), s)
            return f, s, dg + both, ds + gm

        for t, (f, s, dg, ds) in enumerate(lane_tiles(sums, (zero, zero, zero, zero))):
            b_send[ch, :, pl.ds(t * LANES, LANES)] = f
            b_send[ch, :, pl.ds((2 + t) * LANES, LANES)] = s
            grads = (grads[0] + dg, grads[1] + ds)
        for j in range(1, n_chan):
            remote(b_send.at[ch], b_recv.at[ch, j], bs_sem.at[ch, j], br_sem.at[ch, j], me_d, chan_peer(j)).start()
        if ch == 0:
            pair_done(1)

    mine = jnp.concatenate([jnp.sum(v, axis=0, keepdims=True) for v in grads], axis=0)
    d_send[...] = mine
    d_recv[me_d] = mine
    for j in range(1, n_dp):
        remote(d_send, d_recv.at[me_d], ds_sem.at[j], dr_sem.at[me_d], dp_peer(j), me_c).start()
    group_done(0)

    for ch in range(chunks):
        total = b_send[ch]
        for j in range(1, n_chan):
            remote(b_send.at[ch], b_recv.at[ch, j], bs_sem.at[ch, j], br_sem.at[ch, j], me_d, chan_peer(j)).wait_recv()
            total = total + b_recv[ch, j]
        inv = inv_d[ch]
        f = total[:, : 2 * LANES] * inv / width
        s = total[:, 2 * LANES :] * inv / width

        for t in range(2):
            lo = t * LANES
            count = min(LANES, patches - lo)
            cut = slice(lo, lo + LANES)

            def finish(q, carry, ch=ch, lo=lo):
                i_t, f_t, s_t = carry
                for i in range(4):
                    p = lo + q * 4 + i
                    rows = pl.ds(pl.multiple_of(p * NB, NB), NB)
                    bs = pl.ds(ch * NB, NB)
                    gn = gm_n[ch, rows, :] * gain
                    v = u_v[p, bs, :].astype(F32) + column(i_t, i) * gn - column(f_t, i) - column(s_t, i) * normed_n[ch, rows, :]
                    out_ref[p, bs, :] = v.astype(BF16)
                return tuple(pltpu.roll(c, LANES - 4, 1) for c in carry)

            lax.fori_loop(0, count // 4, finish, (inv[:, cut], f[:, cut], s[:, cut]))

    group_done(1)
    all_done(0)
    for j in range(1, n_dp):
        d = dp_peer(j)
        remote(d_send, d_recv.at[d], ds_sem.at[j], dr_sem.at[d], d, me_c).wait_recv()
    vec = d_recv[0]
    for d in range(1, n_dp):
        vec = vec + d_recv[d]
    vec_ref[...] = vec * scale
    all_done(1)

    for ch in range(chunks):
        for j in range(1, n_chan):
            remote(a_send.at[ch], a_recv.at[ch, j], as_sem.at[ch, j], ar_sem.at[ch, j], me_d, chan_peer(j)).wait_send()
            remote(b_send.at[ch], b_recv.at[ch, j], bs_sem.at[ch, j], br_sem.at[ch, j], me_d, chan_peer(j)).wait_send()
    for h in range(2):
        for j in range(1, groups):
            c1(h, j).wait_send()
        for j in range(1, n_chan):
            c2(h, j).wait_send()
    for j in range(1, n_dp):
        remote(d_send, d_recv.at[me_d], ds_sem.at[j], dr_sem.at[me_d], dp_peer(j), me_c).wait_send()


def by_owner(w, groups):
    hid, n = w.shape
    r = hid // (groups * 4)
    return w.reshape(groups, 2, 2, r, n).transpose(2, 0, 1, 3, 4).reshape(hid, n)


def per_device(n_dp, n_chan, inputs, norm_gain, norm_bias, w_first, b_first, w_second, upstream):
    images, patches, local = inputs.shape
    hid = w_first.shape[0]
    groups = n_dp // 2
    chunks = images // NB
    width = float(local * n_chan)
    scale = 1.0 / (images * n_dp)
    hi = lax.reduce_precision(b_first, 8, 7)
    mid = lax.reduce_precision(b_first - hi, 8, 7)
    low = b_first - hi - mid
    cols = jnp.stack([hi, mid, low], axis=1).astype(BF16)
    w1 = by_owner(w_first, groups)
    pad = jnp.zeros((hid, PP - patches - 3), BF16)
    w1a = jnp.concatenate([w1, by_owner(cols, groups), pad], axis=1)
    w1t = w1.T
    w2t = jnp.pad(by_owner(w_second.T, groups), ((0, 0), (0, PP - patches)))
    rows = hid // (groups * 4)
    stat = (chunks, NB, 4 * LANES)
    vmem = pl.BlockSpec(memory_space=pltpu.VMEM)
    hbm = pl.BlockSpec(memory_space=pl.ANY)
    dma = pltpu.SemaphoreType.DMA
    out, first, second, vec = pl.pallas_call(
        functools.partial(kernel, n_dp, n_chan, patches, width, scale),
        out_shape=(
            jax.ShapeDtypeStruct((patches, images, local), BF16),
            jax.ShapeDtypeStruct((2 * rows, 256), F32),
            jax.ShapeDtypeStruct((2 * rows, patches), F32),
            jax.ShapeDtypeStruct((2, local), F32),
        ),
        in_specs=[hbm, hbm] + [vmem] * 5,
        out_specs=(vmem, vmem, vmem, vmem),
        scratch_shapes=[
            pltpu.VMEM((patches, images, local), BF16),
            pltpu.VMEM((patches, images, local), BF16),
            pltpu.VMEM((PP, images * local), BF16),
            pltpu.VMEM((PP, images * local), BF16),
            pltpu.VMEM((hid, images * local), F32),
            pltpu.VMEM((hid, images * local), BF16),
            pltpu.VMEM((hid // 2, NB * local), BF16),
            pltpu.VMEM((chunks, patches * NB, local), F32),
            pltpu.VMEM((chunks, patches * NB, local), F32),
            pltpu.VMEM((16 * NB, local), F32),
            pltpu.VMEM((chunks, NB, 2 * LANES), F32),
            pltpu.VMEM((2, groups, 2, rows, 4 * LANES), F32),
            pltpu.VMEM(stat, F32),
            pltpu.VMEM((chunks, n_chan, NB, 4 * LANES), F32),
            pltpu.VMEM(stat, F32),
            pltpu.VMEM((chunks, n_chan, NB, 4 * LANES), F32),
            pltpu.VMEM((2, groups, rows, 4 * LANES), F32),
            pltpu.VMEM((2, groups, rows, 4 * LANES), F32),
            pltpu.VMEM((2, groups, rows, 4 * LANES), F32),
            pltpu.VMEM((2, rows, 4 * LANES), F32),
            pltpu.VMEM((2, n_chan, rows, 4 * LANES), F32),
            pltpu.VMEM((2, local), F32),
            pltpu.VMEM((n_dp, 2, local), F32),
            dma((2, chunks)),
            dma((chunks, n_chan)),
            dma((chunks, n_chan)),
            dma((chunks, n_chan)),
            dma((chunks, n_chan)),
            dma((2,)),
            dma((2,)),
            dma((2, groups)),
            dma((2, groups)),
            dma((2, n_chan)),
            dma((2, n_chan)),
            dma((n_dp,)),
            dma((n_dp,)),
        ],
        compiler_params=pltpu.CompilerParams(
            collective_id=0, has_side_effects=True, vmem_limit_bytes=64_000_000
        ),
    )(
        inputs.transpose(1, 0, 2),
        upstream.transpose(1, 0, 2),
        norm_gain.reshape(1, local),
        norm_bias.reshape(1, local),
        w1a,
        w1t,
        w2t,
    )
    return (
        out.transpose(1, 0, 2),
        first[:, :patches],
        second.T,
        first[:, patches],
        vec[0],
        vec[1],
    )


def solution(mesh):
    in_specs = (P("dp", None, "chan"), P("chan"), P("chan"), P(), P(), P(), P("dp", None, "chan"))
    out_specs = (P("dp", None, "chan"), P("dp", None), P(None, "dp"), P("dp"), P("chan"), P("chan"))
    body = functools.partial(per_device, mesh.shape["dp"], mesh.shape["chan"])
    return jax.shard_map(
        body, mesh=mesh, in_specs=in_specs, out_specs=out_specs, check_vma=False
    )
```

time: 145 us -> 113 us (0.78)
  Pallas kernels: 0 us -> 98 us
  waiting for transfers between devices: 34 us -> 0 us
  starting transfers between devices: 25.4 us -> 0 us
  other arithmetic: 26.3 us -> 1.62 us
  matrix products: 24.1 us -> 0 us
  blocking collectives: 18.6 us -> 0 us
  local copies, waits for them, and re-layouts: 14.6 us -> 11 us
    pallas_call x0 -> x1, Pallas kernels: none -> 98 us  [per_device(): pl.pallas_call(functools.partial(kernel, n_dp, n_chan, patches, width, sc...]
    all_to_all x4 -> x0, waiting for transfers between devices: 34 us -> none  [the longest x1 27 us: sum_at_owner(): lax.all_to_all(pieces, axis, split_axis=0, concat_axis=0, tiled=True)]
    all_to_all x4 -> x0, starting transfers between devices: 25.4 us -> none  [the longest x3 20.7 us: copy_for_each(): return lax.all_to_all(copies, axis, split_axis=0, concat_axis=0, tiled=True)]
    dot_general x5 -> x0, matrix products: 24.1 us -> none  [the longest x1 7.76 us: per_device(): jnp.einsum('pk,bpc->bkc', w_second, upstream, preferred_element_type=jnp....]
    all_to_all x1 -> x0, blocking collectives: 18.6 us -> none  [copy_for_each(): return lax.all_to_all(copies, axis, split_axis=0, concat_axis=0, tiled=True)]
    reduce_sum x7 -> x0, other arithmetic: 15.2 us -> none  [the longest x1 6.94 us: per_device(): jnp.sum(grad_mixed * normed, axis=(0, 1)) * scale]
    convert_element_type x1 -> x0, other arithmetic: 8.16 us -> none  [per_device(): grad_input = (upstream.astype(jnp.float32) + inv_std * (grad_normed - fir...]
    mul x4 -> x0, local copies, waits for them, and re-layouts: 3.34 us -> none  [the longest x1 1.99 us: per_device(): jnp.einsum('bkc,bpc->kp', grad_pre, mixed_in, preferred_element_type=jnp....]
  transfers between devices with their start and end apart: 4 -> 0, of which waited for: 3 -> 0; matrix products, arithmetic and copies ran while one was open for 17% -> 0% of each run, Pallas kernels for 0% -> 0%
where the time goes in v1:
time: 113 us; the launch traced here: 111 us
  Pallas kernels  98 us (87%)
  local copies, waits for them, and re-layouts  11 us (10%)
  other arithmetic  1.62 us (1%)
    pallas_call x1, Pallas kernels, per_device(): pl.pallas_call(functools.partial(kernel, n_dp, n_chan, patches, width, sc...  98 us
    unnamed x11, local copies, waits for them, and re-layouts  5.95 us

profile of v1, /device:TPU:2, one launch (start us, length us, event | category | flops | bytes accessed | tf_op | source)
XLA Modules:
  0.0 111.2 jit_solution(6936082751891539656)
XLA Ops:
  0.6 0.0 copy-start
  0.7 0.1 pad.7.clone
  0.7 0.7 reduce-precision_convert_fusion.1
  1.4 0.1 stack.12
  1.5 0.1 stack.14
  1.6 0.1 stack.13
  1.7 0.1 maximum_bitcast_fusion
  1.8 0.5 copy.23
  2.3 1.1 copy.16
  3.4 0.8 maximum_maximum_fusion.w1a_ref
  4.2 0.8 copy.20
  5.0 0.0 copy-done
  5.0 0.1 copy.21
  5.2 0.7 pad.4.w2t_ref
  5.9 98.0 %shard_map.118 = (bf16[196,48,128]{2,1,0:T(8,128)(2,1)}, f32[16,256]{1,0:T(8,128)}, f32[16,196]{1,0:T(8,128)}, f32[2,128]{1,0:T(2,128)}) custom-call(bf16[196,48,128]{2,1,0:T(8,128)(2,1)} %bitcast.25, bf16[196,48,128]{2,1,0:T(8,128)(2,1)} %bitcast.26, f32[1,128]{1,0:T(1,128)} %bitcast.37, f32[1,128]{1,0:T(1,128)} %bitcast.38, ...), custom_call_target="tpu_custom_call" | custom-call | tf_op jit(solution)/shard_map/pallas_call | solution.py:383
  103.9 1.4 %slice_reduce_fusion = f32[16]{0:T(128)} fusion(f32[16,256]{1,0:T(8,128)} %get-tuple-element.11), kind=kLoop, calls=%fused_computation.2 | loop fusion | bytes 128 | tf_op jit(solution)/shard_map/slice | solution.py:447
  105.3 1.2 %slice_bitcast_fusion = (f32[128]{0:T(128)}, f32[128]{0:T(128)}) fusion(f32[2,128]{1,0:T(2,128)} %get-tuple-element.13), kind=kLoop, calls=%fused_computation.8 | loop fusion | bytes 2048 | tf_op jit(solution)/shard_map/squeeze | solution.py:449
  106.5 0.0 copy-start.1
  106.5 0.0 copy-start.2
  106.5 3.5 %copy.28 = bf16[48,196,128]{2,0,1:T(8,128)(2,1)} copy(bf16[48,196,128]{2,0,1:T(8,128)(2,1)} %bitcast.27) | data formatting | bytes 4816896
  110.0 0.0 copy-done.1
  110.0 0.6 copy.29
  110.6 0.0 copy-done.2
  110.6 0.6 copy.30
  (3 shorter events, 0.0 us)
Async XLA Ops:
  0.6 4.4 %copy-start = (bf16[196,512]{1,0:T(8,128)(2,1)S(1)}, bf16[196,512]{1,0:T(8,128)(2,1)}, u32[]{:S(2)}) copy-start(bf16[196,512]{1,0:T(8,128)(2,1)} %param.12) | copy-start | bytes 602116
  106.5 3.5 %copy-start.1 = (f32[16,256]{1,0:T(8,128)S(1)}, f32[16,256]{1,0:T(8,128)}, u32[]{:S(2)}) copy-start(f32[16,256]{1,0:T(8,128)} %get-tuple-element.11) | copy-start | bytes 49156
  106.5 4.1 %copy-start.2 = (f32[16,196]{1,0:T(8,128)S(1)}, f32[16,196]{1,0:T(8,128)}, u32[]{:S(2)}) copy-start(f32[16,196]{1,0:T(8,128)} %get-tuple-element.12) | copy-start | bytes 37636

commit v2 on v1

--- a/solution.py
+++ b/solution.py
@@ -11,6 +11,10 @@
 NB = 16
 PP = 208
 LANES = 128
+UG = 4
+VMEM_LIMIT = 52_000_000
+UH = 4
+UB = 4
 F32 = jnp.float32
 BF16 = jnp.bfloat16
 
@@ -21,8 +25,9 @@
 
 def kernel(
     n_dp, n_chan, patches, width, scale,
-    x_hbm, u_hbm, gain_ref, bias_ref, w1a_ref, w1t_ref, w2t_ref,
-    out_ref, first_ref, second_ref, vec_ref,
+    x_hbm, u_hbm, gain_ref, bias_ref, w1_ref, bf_ref, w2_ref,
+    out_ref, first_ref, second_ref, first_b_ref, gain_g_ref, shift_g_ref,
+    w1f, w2f, wtail, w1a, w1t, w2t,
     x_v, u_v, mx, up, ga, gp, act, normed_n, gm_n, tmp, inv_d, acc,
     a_send, a_recv, b_send, b_recv, p0_recv, csum, c1_recv, c1_sum, c2_recv, d_send, d_recv,
     load_sem, as_sem, ar_sem, bs_sem, br_sem, p0s_sem, p0r_sem, c1s_sem, c1r_sem, c2s_sem, c2r_sem, ds_sem, dr_sem,
@@ -33,7 +38,7 @@
     me_g = lax.div(me_d, 2)
     groups = n_dp // 2
     chunks = x_v.shape[1] // NB
-    hid = w1a_ref.shape[0]
+    hid = w1_ref.shape[1]
     half = hid // 2
     tiles = NB // 2
     span = NB * LANES
@@ -56,14 +61,15 @@
     for j in range(1, n_dp):
         pl.semaphore_signal(barrier, inc=1, device_id={"dp": dp_peer(j), "chan": me_c}, device_id_type=pl.DeviceIdType.MESH)
 
-    def load(which, src, dst, ch):
-        rows = pl.ds(ch * NB, NB)
-        return pltpu.make_async_copy(src.at[:, rows, :], dst.at[:, rows, :], load_sem.at[which, ch])
-
-    for ch in range(chunks):
-        load(0, x_hbm, x_v, ch).start()
-    for ch in range(chunks):
-        load(1, u_hbm, u_v, ch).start()
+    def load(which, src, dst, part):
+        lo = part * 64
+        rows = pl.ds(lo, 64 if part < 2 else patches - lo)
+        return pltpu.make_async_copy(src.at[rows], dst.at[rows], load_sem.at[which, part])
+
+    for part in range(3):
+        load(0, x_hbm, x_v, part).start()
+    for part in range(3):
+        load(1, u_hbm, u_v, part).start()
 
     lane = lax.broadcasted_iota(jnp.int32, (NB, LANES), 1)
 
@@ -71,35 +77,73 @@
         out = []
         for lo in range(0, patches, LANES):
             count = min(LANES, patches - lo)
-
-            def step(q, carry, lo=lo):
-                for i in range(4):
-                    carry = body(lo + q * 4 + i, q * 4 + i, carry)
+            unroll = 32 if count == LANES else 34
+
+            def step(q, carry, lo=lo, unroll=unroll):
+                for i in range(unroll):
+                    carry = body(lo + q * unroll + i, q * unroll + i, carry)
                 return carry
 
-            out.append(lax.fori_loop(0, count // 4, step, init))
+            out.append(lax.fori_loop(0, count // unroll, step, init))
         return out
 
     zero = jnp.zeros((NB, LANES), F32)
 
-    for ch in range(chunks):
-        load(0, x_hbm, x_v, ch).wait()
-
-        def stat(p, at, carry, ch=ch):
-            s, q = carry
-            v = x_v[p, pl.ds(ch * NB, NB), :].astype(F32)
-            hit = lane == at
-            s = jnp.where(hit, jnp.sum(v, axis=-1, keepdims=True), s)
-            q = jnp.where(hit, jnp.sum(v * v, axis=-1, keepdims=True), q)
-            return s, q
-
-        for t, (s, q) in enumerate(lane_tiles(stat, (zero, zero))):
-            a_send[ch, :, pl.ds(t * LANES, LANES)] = s
-            a_send[ch, :, pl.ds((2 + t) * LANES, LANES)] = q
-        if ch == 0:
-            pl.semaphore_wait(barrier, n_chan - 1 + n_dp - 1)
+    images = x_v.shape[1]
+    wide = lax.broadcasted_iota(jnp.int32, (images, LANES), 1)
+    stats = (jnp.zeros((images, LANES), F32),) * 2
+    for part in range(3):
+        load(0, x_hbm, x_v, part).wait()
+        lo = part * 64
+        unroll = 16 if part < 2 else 17
+        count = (64 if part < 2 else patches - lo) // unroll
+
+        def stat(q, carry, lo=lo, unroll=unroll):
+            s, sq = carry
+            for i in range(unroll):
+                p = lo + q * unroll + i
+                v = x_v[p].astype(F32)
+                hit = wide == lax.rem(p, LANES)
+                s = jnp.where(hit, jnp.sum(v, axis=-1, keepdims=True), s)
+                sq = jnp.where(hit, jnp.sum(v * v, axis=-1, keepdims=True), sq)
+            return s, sq
+
+        stats = lax.fori_loop(0, count, stat, stats)
+        if part:
+            t = part - 1
+            for ch in range(chunks):
+                a_send[ch, :, pl.ds(t * LANES, LANES)] = stats[0][ch * NB : (ch + 1) * NB]
+                a_send[ch, :, pl.ds((2 + t) * LANES, LANES)] = stats[1][ch * NB : (ch + 1) * NB]
+    pl.semaphore_wait(barrier, n_chan - 1 + n_dp - 1)
+    for ch in range(chunks):
         for j in range(1, n_chan):
             remote(a_send.at[ch], a_recv.at[ch, j], as_sem.at[ch, j], ar_sem.at[ch, j], me_d, chan_peer(j)).start()
+
+    def select(lo, count):
+        at = lo + lax.broadcasted_iota(jnp.int32, (count, hid), 0)
+        h, rest_ = at // half, at % half
+        unit = rest_ // 8 * 16 + h * 8 + rest_ % 8
+        return jnp.where(lax.broadcasted_iota(jnp.int32, (count, hid), 1) == unit, 1.0, 0.0).astype(BF16)
+
+    tail = patches // 16 * 16
+    left = patches - tail
+    for ref, dst in ((w1_ref, w1f), (w2_ref, w2f)):
+        dst[pl.ds(0, tail), :] = ref[pl.ds(0, tail), :]
+        wtail[...] = jnp.zeros((16, hid), F32)
+        wtail[pl.ds(0, left), :] = ref[pl.ds(tail, left), :].astype(F32)
+        if ref is w1_ref:
+            rem = bf_ref[...]
+            for i in range(3):
+                piece = rem.astype(BF16).astype(F32)
+                wtail[pl.ds(left + i, 1), :] = piece
+                rem = rem - piece
+        dst[pl.ds(tail, 16), :] = wtail[...].astype(BF16)
+    for h in range(2):
+        pick = select(h * half, half)
+        rows = pl.ds(h * half, half)
+        w1a[rows, :] = contract_lanes(pick, w1f[...]).astype(BF16)
+        w2t[rows, :] = contract_lanes(pick, w2f[...]).astype(BF16)
+        w1t[:, rows] = contract_lanes(w1f[pl.ds(0, patches), :], pick).astype(BF16)
 
     def regroup(g, ch, dst, value, fill):
         for i in range(16):
@@ -116,8 +160,9 @@
     rest = patches - full * 16
     sub = lax.broadcasted_iota(jnp.int32, (16, LANES), 0)
 
-    for ch in range(chunks):
-        load(1, u_hbm, u_v, ch).wait()
+    for part in range(3):
+        load(1, u_hbm, u_v, part).wait()
+    for ch in range(chunks):
 
         def up_group(g, _, ch=ch):
             regroup(g, ch, up, lambda i: u_v[g * 16 + i, pl.ds(ch * NB, NB), :].astype(F32), None)
@@ -132,10 +177,12 @@
 
     def ga_tile(n, _):
         at = pl.ds(pl.multiple_of(n * 256, 256), 256)
-        ga[:, at] = jnp.dot(w2t_ref[...], up[:, at], preferred_element_type=F32)
+        ga[:, at] = jnp.dot(w2t[...], up[:, at], preferred_element_type=F32)
         return 0
 
-    lax.fori_loop(0, chunks * tiles, ga_tile, 0)
+    lax.fori_loop(0, chunks * tiles, ga_tile, 0, unroll=UG)
+
+    owned_b = []
 
     gain = gain_ref[...]
     bias = bias_ref[...]
@@ -189,7 +236,7 @@
 
         def tile(n, _):
             at = pl.ds(pl.multiple_of(ch * span + n * 256, 256), 256)
-            pre = jnp.dot(w1a_ref[rows, :], mx[:, at], preferred_element_type=F32)
+            pre = jnp.dot(w1a[rows, :], mx[:, at], preferred_element_type=F32)
             t = pre * 0.7071067811865476
             cdf = 0.5 * lax.erf(t) + 0.5
             act[:, pl.ds(pl.multiple_of(n * 256, 256), 256)] = (pre * cdf).astype(BF16)
@@ -197,7 +244,7 @@
             gp[rows, at] = (ga[rows, at] * slope).astype(BF16)
             return 0
 
-        lax.fori_loop(0, tiles, tile, 0)
+        lax.fori_loop(0, tiles, tile, 0, unroll=UH)
         at = pl.ds(ch * span, span)
         first = contract_lanes(gp[rows, at], mx[:, at]).reshape(groups, 2, -1, PP)
         second = contract_lanes(act[...], up[:, at]).reshape(groups, 2, -1, PP)
@@ -250,11 +297,14 @@
         for c in range(1, n_chan):
             total = total + c2_recv[h, c]
         total = total * scale
-        first_ref[pl.ds(h * 8, 8), :] = total[:, :256]
+        first_ref[pl.ds(h * 8, 8), :] = total[:, :patches]
+        here = lax.broadcasted_iota(jnp.int32, (8, LANES), 0) + h * 8 == lax.broadcasted_iota(jnp.int32, (8, LANES), 1)
+        owned_b.append(jnp.sum(jnp.where(here, total[:, patches : patches + 1], 0.0), axis=0, keepdims=True))
         second_ref[pl.ds(h * 8, 8), :] = total[:, 256 : 256 + patches]
 
     for ch in range(chunks):
         normalise(ch)
+    for ch in range(chunks):
         hidden(0, ch)
     p0(0).start()
     for ch in range(chunks):
@@ -268,12 +318,12 @@
 
         def back(n, _, ch=ch):
             at = pl.ds(pl.multiple_of(ch * span + n * 256, 256), 256)
-            gm = jnp.dot(w1t_ref[...], gp[:, at], preferred_element_type=F32)
+            gm = jnp.dot(w1t[...], gp[:, at], preferred_element_type=F32)
             for i in range(2):
                 gm_n[ch, pl.ds(n * 2 + i, patches, stride=NB), :] = gm[:, i * LANES : (i + 1) * LANES]
             return 0
 
-        lax.fori_loop(0, tiles, back, 0)
+        lax.fori_loop(0, tiles, back, 0, unroll=UB)
 
         def sums(p, at, carry, ch=ch):
             f, s, dg, ds = carry
@@ -316,18 +366,20 @@
             count = min(LANES, patches - lo)
             cut = slice(lo, lo + LANES)
 
-            def finish(q, carry, ch=ch, lo=lo):
+            unroll = 32 if count == LANES else 34
+
+            def finish(q, carry, ch=ch, lo=lo, unroll=unroll):
                 i_t, f_t, s_t = carry
-                for i in range(4):
-                    p = lo + q * 4 + i
+                for i in range(unroll):
+                    p = lo + q * unroll + i
                     rows = pl.ds(pl.multiple_of(p * NB, NB), NB)
                     bs = pl.ds(ch * NB, NB)
                     gn = gm_n[ch, rows, :] * gain
                     v = u_v[p, bs, :].astype(F32) + column(i_t, i) * gn - column(f_t, i) - column(s_t, i) * normed_n[ch, rows, :]
                     out_ref[p, bs, :] = v.astype(BF16)
-                return tuple(pltpu.roll(c, LANES - 4, 1) for c in carry)
-
-            lax.fori_loop(0, count // 4, finish, (inv[:, cut], f[:, cut], s[:, cut]))
+                return tuple(pltpu.roll(c, LANES - unroll, 1) for c in carry)
+
+            lax.fori_loop(0, count // unroll, finish, (inv[:, cut], f[:, cut], s[:, cut]))
 
     group_done(1)
     all_done(0)
@@ -337,8 +389,10 @@
     vec = d_recv[0]
     for d in range(1, n_dp):
         vec = vec + d_recv[d]
-    vec_ref[...] = vec * scale
+    gain_g_ref[...] = vec[0:1] * scale
+    shift_g_ref[...] = vec[1:2] * scale
     all_done(1)
+    first_b_ref[...] = (owned_b[0] + owned_b[1])[:, :16]
 
     for ch in range(chunks):
         for j in range(1, n_chan):
@@ -351,12 +405,6 @@
             c2(h, j).wait_send()
     for j in range(1, n_dp):
         remote(d_send, d_recv.at[me_d], ds_sem.at[j], dr_sem.at[me_d], dp_peer(j), me_c).wait_send()
-
-
-def by_owner(w, groups):
-    hid, n = w.shape
-    r = hid // (groups * 4)
-    return w.reshape(groups, 2, 2, r, n).transpose(2, 0, 1, 3, 4).reshape(hid, n)
 
 
 def per_device(n_dp, n_chan, inputs, norm_gain, norm_bias, w_first, b_first, w_second, upstream):
@@ -366,31 +414,30 @@
     chunks = images // NB
     width = float(local * n_chan)
     scale = 1.0 / (images * n_dp)
-    hi = lax.reduce_precision(b_first, 8, 7)
-    mid = lax.reduce_precision(b_first - hi, 8, 7)
-    low = b_first - hi - mid
-    cols = jnp.stack([hi, mid, low], axis=1).astype(BF16)
-    w1 = by_owner(w_first, groups)
-    pad = jnp.zeros((hid, PP - patches - 3), BF16)
-    w1a = jnp.concatenate([w1, by_owner(cols, groups), pad], axis=1)
-    w1t = w1.T
-    w2t = jnp.pad(by_owner(w_second.T, groups), ((0, 0), (0, PP - patches)))
     rows = hid // (groups * 4)
     stat = (chunks, NB, 4 * LANES)
     vmem = pl.BlockSpec(memory_space=pltpu.VMEM)
-    hbm = pl.BlockSpec(memory_space=pl.ANY)
+    hbm = pl.BlockSpec(memory_space=pltpu.HBM)
     dma = pltpu.SemaphoreType.DMA
-    out, first, second, vec = pl.pallas_call(
+    out, first, second, first_b, gain_g, shift_g = pl.pallas_call(
         functools.partial(kernel, n_dp, n_chan, patches, width, scale),
         out_shape=(
             jax.ShapeDtypeStruct((patches, images, local), BF16),
-            jax.ShapeDtypeStruct((2 * rows, 256), F32),
             jax.ShapeDtypeStruct((2 * rows, patches), F32),
-            jax.ShapeDtypeStruct((2, local), F32),
+            jax.ShapeDtypeStruct((2 * rows, patches), F32),
+            jax.ShapeDtypeStruct((1, 2 * rows), F32),
+            jax.ShapeDtypeStruct((1, local), F32),
+            jax.ShapeDtypeStruct((1, local), F32),
         ),
         in_specs=[hbm, hbm] + [vmem] * 5,
-        out_specs=(vmem, vmem, vmem, vmem),
+        out_specs=(vmem,) * 6,
         scratch_shapes=[
+            pltpu.VMEM((PP, hid), BF16),
+            pltpu.VMEM((PP, hid), BF16),
+            pltpu.VMEM((16, hid), F32),
+            pltpu.VMEM((hid, PP), BF16),
+            pltpu.VMEM((patches, hid), BF16),
+            pltpu.VMEM((hid, PP), BF16),
             pltpu.VMEM((patches, images, local), BF16),
             pltpu.VMEM((patches, images, local), BF16),
             pltpu.VMEM((PP, images * local), BF16),
@@ -414,7 +461,7 @@
             pltpu.VMEM((2, n_chan, rows, 4 * LANES), F32),
             pltpu.VMEM((2, local), F32),
             pltpu.VMEM((n_dp, 2, local), F32),
-            dma((2, chunks)),
+            dma((2, 3)),
             dma((chunks, n_chan)),
             dma((chunks, n_chan)),
             dma((chunks, n_chan)),
@@ -429,24 +476,24 @@
             dma((n_dp,)),
         ],
         compiler_params=pltpu.CompilerParams(
-            collective_id=0, has_side_effects=True, vmem_limit_bytes=64_000_000
+            collective_id=0, has_side_effects=True, vmem_limit_bytes=VMEM_LIMIT
         ),
     )(
         inputs.transpose(1, 0, 2),
         upstream.transpose(1, 0, 2),
         norm_gain.reshape(1, local),
         norm_bias.reshape(1, local),
-        w1a,
-        w1t,
-        w2t,
+        w_first.T,
+        b_first.reshape(1, hid),
+        w_second,
     )
     return (
         out.transpose(1, 0, 2),
-        first[:, :patches],
+        first,
         second.T,
-        first[:, patches],
-        vec[0],
-        vec[1],
+        first_b[0],
+        gain_g[0],
+        shift_g[0],
     )
 
 

time: 113 us -> 75.2 us (0.67); the launches traced: 111 us -> 75 us
  Pallas kernels: 98 us -> 66.4 us
  local copies, waits for them, and re-layouts: 11 us -> 8.01 us
  other arithmetic: 1.62 us -> 0 us
    pallas_call x1, Pallas kernels: 98 us -> 66.4 us  [per_device(): pl.pallas_call(functools.partial(kernel, n_dp, n_chan, patches, width, sc...]
    unnamed x11 -> x16, local copies, waits for them, and re-layouts: 5.95 us -> 8.01 us
    slice x1 -> x0, local copies, waits for them, and re-layouts: 1.39 us -> none  [per_device(): first[:, patches]]
    reshape x2 -> x0, local copies, waits for them, and re-layouts: 1.27 us -> none  [by_owner(): w.reshape(groups, 2, 2, r, n).transpose(2, 0, 1, 3, 4).reshape(hid, n)]
    squeeze x1 -> x0, local copies, waits for them, and re-layouts: 1.2 us -> none  [per_device(): vec[1]]
where the time goes in v2:
time: 75.2 us; the launch traced here: 75 us
  Pallas kernels  66.4 us (88%)
  local copies, waits for them, and re-layouts  8.01 us (11%)
    pallas_call x1, Pallas kernels, per_device(): pl.pallas_call(functools.partial(kernel, n_dp, n_chan, patches, width, sc...  66.4 us
    unnamed x16, local copies, waits for them, and re-layouts  8.01 us

profile of v2, /device:TPU:2, one launch (start us, length us, event | category | flops | bytes accessed | tf_op | source)
XLA Modules:
  0.0 75.0 jit_solution(15279780899075969962)
XLA Ops:
  0.6 0.0 copy-start
  0.6 0.9 %copy-done = bf16[512,196]{0,1:T(8,128)(2,1)S(1)} copy-done((bf16[512,196]{0,1:T(8,128)(2,1)S(1)}, bf16[512,196]{0,1:T(8,128)(2,1)}, u32[]{:S(2)}) %copy-start) | copy-done | bytes 200728
  1.6 0.0 copy-start.1
  1.6 0.9 %copy-done.1 = bf16[196,512]{1,0:T(8,128)(2,1)S(1)} copy-done((bf16[196,512]{1,0:T(8,128)(2,1)S(1)}, bf16[196,512]{1,0:T(8,128)(2,1)}, u32[]{:S(2)}) %copy-start.1) | copy-done | bytes 200728
  2.5 0.0 copy-start.2
  2.5 0.7 copy-done.2
  3.2 0.0 copy-start.3
  3.2 0.7 copy-done.3
  3.8 0.0 copy-start.4
  3.8 0.7 copy-done.4
  4.5 66.4 %shard_map.118 = (bf16[196,48,128]{2,1,0:T(8,128)(2,1)S(1)}, f32[16,196]{1,0:T(8,128)S(1)}, f32[16,196]{1,0:T(8,128)S(1)}, f32[1,16]{1,0:T(1,128)S(1)}, f32[1,128]{1,0:T(1,128)S(1)}, /*index=5*/f32[1,128]{1,0:T(1,128)S(1)}) custom-call(bf16[196,48,128]{2,1,0:T(8,128)(2,1)} %bitcast.20, bf16[196,48,128]{2,1,0:T(8,128)(2,1)} %bitcast.21, ...), custom_call_target="tpu_custom_call" | custom-call | tf_op jit(solution)/shard_map/pallas_call | solution.py:422
  70.9 1.4 %copy.19 = bf16[48,196,128]{2,0,1:T(8,128)(2,1)} copy(bf16[48,196,128]{2,0,1:T(8,128)(2,1)S(1)} %bitcast.11) | data formatting | bytes 4816896
  72.3 0.6 copy.20
  72.9 0.6 copy.21
  73.5 0.5 copy.22
  74.0 0.5 copy.23
  74.5 0.5 copy.24
Async XLA Ops:
  0.6 0.9 %copy-start = (bf16[512,196]{0,1:T(8,128)(2,1)S(1)}, bf16[512,196]{0,1:T(8,128)(2,1)}, u32[]{:S(2)}) copy-start(bf16[512,196]{0,1:T(8,128)(2,1)} %param.10) | copy-start | bytes 602116
  1.6 0.9 %copy-start.1 = (bf16[196,512]{1,0:T(8,128)(2,1)S(1)}, bf16[196,512]{1,0:T(8,128)(2,1)}, u32[]{:S(2)}) copy-start(bf16[196,512]{1,0:T(8,128)(2,1)} %w2_ref.1) | copy-start | bytes 602116
  2.5 0.7 copy-start.2
  3.2 0.7 copy-start.3
  3.8 0.7 copy-start.4

commit v3 on v2

--- a/solution.py
+++ b/solution.py
@@ -11,10 +11,13 @@
 NB = 16
 PP = 208
 LANES = 128
-UG = 4
-VMEM_LIMIT = 52_000_000
-UH = 4
-UB = 4
+UG = 8
+US = 4
+UN = 6
+UR = 8
+UF = 8
+VMEM_LIMIT = 51_500_000
+UH = 8
 F32 = jnp.float32
 BF16 = jnp.bfloat16
 
@@ -25,12 +28,12 @@
 
 def kernel(
     n_dp, n_chan, patches, width, scale,
-    x_hbm, u_hbm, gain_ref, bias_ref, w1_ref, bf_ref, w2_ref,
+    x_hbm, u_hbm, gain_hbm, bias_hbm, w1_hbm, bf_hbm, w2_hbm,
     out_ref, first_ref, second_ref, first_b_ref, gain_g_ref, shift_g_ref,
-    w1f, w2f, wtail, w1a, w1t, w2t,
-    x_v, u_v, mx, up, ga, gp, act, normed_n, gm_n, tmp, inv_d, acc,
+    gain_ref, bias_ref, w1_ref, bf_ref, w2_ref, w1f, w2f, wtail, w1a, w1t, w2t,
+    x_v, u_v, mx, up, ga, gp, act, normed_n, inv_n, gm_n, tmp, mean_d, inv_d, first_d, second_d, acc,
     a_send, a_recv, b_send, b_recv, p0_recv, csum, c1_recv, c1_sum, c2_recv, d_send, d_recv,
-    load_sem, as_sem, ar_sem, bs_sem, br_sem, p0s_sem, p0r_sem, c1s_sem, c1r_sem, c2s_sem, c2r_sem, ds_sem, dr_sem,
+    load_sem, small_sem, as_sem, ar_sem, bs_sem, br_sem, p0s_sem, p0r_sem, c1s_sem, c1r_sem, c2s_sem, c2r_sem, ds_sem, dr_sem,
 ):
     me_d = lax.axis_index("dp")
     me_c = lax.axis_index("chan")
@@ -38,7 +41,7 @@
     me_g = lax.div(me_d, 2)
     groups = n_dp // 2
     chunks = x_v.shape[1] // NB
-    hid = w1_ref.shape[1]
+    hid = w1_hbm.shape[1]
     half = hid // 2
     tiles = NB // 2
     span = NB * LANES
@@ -68,52 +71,62 @@
 
     for part in range(3):
         load(0, x_hbm, x_v, part).start()
+    small = [
+        pltpu.make_async_copy(src, dst, small_sem.at[i])
+        for i, (src, dst) in enumerate(
+            ((w1_hbm, w1_ref), (w2_hbm, w2_ref), (bf_hbm, bf_ref), (gain_hbm, gain_ref), (bias_hbm, bias_ref))
+        )
+    ]
+    for copy in small:
+        copy.start()
     for part in range(3):
         load(1, u_hbm, u_v, part).start()
 
-    lane = lax.broadcasted_iota(jnp.int32, (NB, LANES), 1)
-
-    def lane_tiles(body, init):
-        out = []
-        for lo in range(0, patches, LANES):
-            count = min(LANES, patches - lo)
-            unroll = 32 if count == LANES else 34
-
-            def step(q, carry, lo=lo, unroll=unroll):
-                for i in range(unroll):
-                    carry = body(lo + q * unroll + i, q * unroll + i, carry)
-                return carry
-
-            out.append(lax.fori_loop(0, count // unroll, step, init))
-        return out
-
-    zero = jnp.zeros((NB, LANES), F32)
-
-    images = x_v.shape[1]
-    wide = lax.broadcasted_iota(jnp.int32, (images, LANES), 1)
-    stats = (jnp.zeros((images, LANES), F32),) * 2
+    blocks = -(-patches // 8)
+    second_row = -(-blocks // 8) * 8
+    eye = lax.broadcasted_iota(jnp.int32, (LANES, LANES), 0) == lax.broadcasted_iota(jnp.int32, (LANES, LANES), 1)
+
+    def dense(value):
+        n = value.shape[0]
+        return jnp.sum(jnp.where(eye[:n], value, 0.0), axis=0, keepdims=True)
+
+    def spread(row):
+        return jnp.broadcast_to(row, (LANES, LANES)).T
+
+    def over_blocks(body, init, lo=0, hi=None, unroll=4):
+        hi = blocks if hi is None else hi
+        whole = min(hi, patches // 8) - lo
+
+        def step(i, carry):
+            for k in range(unroll):
+                carry = body(lo + i * unroll + k, LANES, carry)
+            return carry
+
+        carry = lax.fori_loop(0, whole // unroll, step, init)
+        for k in range(whole // unroll * unroll, whole):
+            carry = body(lo + k, LANES, carry)
+        if hi > patches // 8:
+            carry = body(hi - 1, (patches % 8) * NB, carry)
+        return carry
+
+    def images_of(ref, g, n, ch):
+        return ref[pl.ds(g * 8, n // NB), pl.ds(ch * NB, NB), :].reshape(n, LANES)
+
+    ones = jnp.ones((LANES, LANES), BF16)
     for part in range(3):
         load(0, x_hbm, x_v, part).wait()
-        lo = part * 64
-        unroll = 16 if part < 2 else 17
-        count = (64 if part < 2 else patches - lo) // unroll
-
-        def stat(q, carry, lo=lo, unroll=unroll):
-            s, sq = carry
-            for i in range(unroll):
-                p = lo + q * unroll + i
-                v = x_v[p].astype(F32)
-                hit = wide == lax.rem(p, LANES)
-                s = jnp.where(hit, jnp.sum(v, axis=-1, keepdims=True), s)
-                sq = jnp.where(hit, jnp.sum(v * v, axis=-1, keepdims=True), sq)
-            return s, sq
-
-        stats = lax.fori_loop(0, count, stat, stats)
-        if part:
-            t = part - 1
+
+        def stat(g, n, carry):
             for ch in range(chunks):
-                a_send[ch, :, pl.ds(t * LANES, LANES)] = stats[0][ch * NB : (ch + 1) * NB]
-                a_send[ch, :, pl.ds((2 + t) * LANES, LANES)] = stats[1][ch * NB : (ch + 1) * NB]
+                v = images_of(x_v, g, n, ch)
+                total = jnp.dot(v, ones, preferred_element_type=F32)
+                v = v.astype(F32)
+                a_send[ch, pl.ds(g, 1), :] = dense(total)
+                squares = jnp.broadcast_to(jnp.sum(v * v, axis=-1, keepdims=True), (n, LANES))
+                a_send[ch, pl.ds(second_row + g, 1), :] = dense(squares)
+            return carry
+
+        over_blocks(stat, 0, part * 8, part * 8 + 8 if part < 2 else None, US)
     pl.semaphore_wait(barrier, n_chan - 1 + n_dp - 1)
     for ch in range(chunks):
         for j in range(1, n_chan):
@@ -125,6 +138,8 @@
         unit = rest_ // 8 * 16 + h * 8 + rest_ % 8
         return jnp.where(lax.broadcasted_iota(jnp.int32, (count, hid), 1) == unit, 1.0, 0.0).astype(BF16)
 
+    for copy in small:
+        copy.wait()
     tail = patches // 16 * 16
     left = patches - tail
     for ref, dst in ((w1_ref, w1f), (w2_ref, w2f)):
@@ -145,9 +160,8 @@
         w2t[rows, :] = contract_lanes(pick, w2f[...]).astype(BF16)
         w1t[:, rows] = contract_lanes(w1f[pl.ds(0, patches), :], pick).astype(BF16)
 
-    def regroup(g, ch, dst, value, fill):
-        for i in range(16):
-            tmp[pl.ds(i * NB, NB), :] = value(i)
+    tmp[...] = jnp.zeros_like(tmp)
+    def ungroup(g, ch, dst, fill):
         for b in range(NB):
             v = tmp[pl.ds(b, 16, stride=NB), :]
             if fill is not None:
@@ -165,19 +179,17 @@
     for ch in range(chunks):
 
         def up_group(g, _, ch=ch):
-            regroup(g, ch, up, lambda i: u_v[g * 16 + i, pl.ds(ch * NB, NB), :].astype(F32), None)
+            tmp[...] = u_v[pl.ds(g * 16, 16), pl.ds(ch * NB, NB), :].reshape(16 * NB, LANES).astype(F32)
+            ungroup(g, ch, up, None)
             return 0
 
         lax.fori_loop(0, full, up_group, 0)
-        regroup(
-            full, ch, up,
-            lambda i, ch=ch: u_v[full * 16 + min(i, rest - 1), pl.ds(ch * NB, NB), :].astype(F32),
-            lambda v: jnp.where(sub < rest, v, 0.0),
-        )
+        tmp[pl.ds(0, rest * NB), :] = images_of(u_v, full * 2, rest * NB, ch).astype(F32)
+        ungroup(full, ch, up, lambda v: jnp.where(sub < rest, v, 0.0))
 
     def ga_tile(n, _):
         at = pl.ds(pl.multiple_of(n * 256, 256), 256)
-        ga[:, at] = jnp.dot(w2t[...], up[:, at], preferred_element_type=F32)
+        ga[:, at] = jnp.dot(w2t[...], up[:, at], preferred_element_type=F32).astype(BF16)
         return 0
 
     lax.fori_loop(0, chunks * tiles, ga_tile, 0, unroll=UG)
@@ -187,49 +199,41 @@
     gain = gain_ref[...]
     bias = bias_ref[...]
 
-    def wait_a(ch):
-        total = a_send[ch]
-        for j in range(1, n_chan):
-            remote(a_send.at[ch], a_recv.at[ch, j], as_sem.at[ch, j], ar_sem.at[ch, j], me_d, chan_peer(j)).wait_recv()
-            total = total + a_recv[ch, j]
-        mean = total[:, : 2 * LANES] / width
-        var = total[:, 2 * LANES :] / width - mean * mean
-        return mean, lax.rsqrt(var + EPS)
-
-    def column(value, i):
-        return jnp.broadcast_to(value[:, i : i + 1], (NB, LANES))
+    def received(send, recv, ssem, rsem, ch):
+        for j in range(1, n_chan):
+            remote(send.at[ch], recv.at[ch, j], ssem.at[ch, j], rsem.at[ch, j], me_d, chan_peer(j)).wait_recv()
+        totals = []
+        for lo in (0, second_row):
+            total = send[ch, pl.ds(lo, blocks), :]
+            for j in range(1, n_chan):
+                total = total + recv[ch, j, pl.ds(lo, blocks), :]
+            totals.append(total)
+        return totals
 
     def normalise(ch):
-        mean, inv = wait_a(ch)
-        inv_d[ch] = inv
-        mean_ref, inv_ref = a_send.at[ch], inv_d.at[ch]
-
-        def one(g, mean16, inv16, count):
-            def value(i):
-                i = min(i, count - 1)
-                p = g * 16 + i
-                v = x_v[p, pl.ds(ch * NB, NB), :].astype(F32)
-                normed = (v - column(mean16, i)) * column(inv16, i)
-                normed_n[ch, pl.ds(pl.multiple_of(p * NB, NB), NB), :] = normed
-                return normed * gain + bias
-
-            fill = None
-            if count < 16:
-                fill = lambda v: jnp.where(sub < rest, v, jnp.where(sub < rest + 3, 1.0, 0.0))
-            regroup(g, ch, mx, value, fill)
-
-        for t in range(2):
-            m_t = mean[:, t * LANES : (t + 1) * LANES]
-            i_t = inv[:, t * LANES : (t + 1) * LANES]
-            per = LANES // 16
-
-            def group(g, carry, t=t):
-                m, v = carry
-                one(t * per + g, m, v, 16)
-                return pltpu.roll(m, LANES - 16, 1), pltpu.roll(v, LANES - 16, 1)
-
-            m_t, i_t = lax.fori_loop(0, min(per, full - t * per), group, (m_t, i_t))
-        one(full, m_t, i_t, rest)
+        total, squares = received(a_send, a_recv, as_sem, ar_sem, ch)
+        mean = total / width
+        mean_d[ch] = mean
+        inv_d[ch] = lax.rsqrt(squares / width - mean * mean + EPS)
+
+        def block(g, n):
+            m = spread(mean_d[ch, pl.ds(g, 1), :])[:n]
+            inv = spread(inv_d[ch, pl.ds(g, 1), :])[:n]
+            rows = pl.ds(pl.multiple_of(g * LANES, 64), n)
+            normed = (images_of(x_v, g, n, ch).astype(F32) - m) * inv
+            normed_n[ch, rows, :] = normed
+            inv_n[ch, rows, :] = inv
+            return normed * gain + bias
+
+        def pair(g, carry):
+            for k in range(2):
+                tmp[pl.ds(k * LANES, LANES), :] = block(g * 2 + k, LANES)
+            ungroup(g, ch, mx, None)
+            return carry
+
+        lax.fori_loop(0, full, pair, 0, unroll=UN)
+        tmp[pl.ds(0, rest * NB), :] = block(blocks - 1, rest * NB)
+        ungroup(full, ch, mx, lambda v: jnp.where(sub < rest, v, jnp.where(sub < rest + 3, 1.0, 0.0)))
 
     def hidden(h, ch):
         rows = pl.ds(h * half, half)
@@ -241,7 +245,7 @@
             cdf = 0.5 * lax.erf(t) + 0.5
             act[:, pl.ds(pl.multiple_of(n * 256, 256), 256)] = (pre * cdf).astype(BF16)
             slope = cdf + (t * 0.5641895835477563) * jnp.exp(-(t * t))
-            gp[rows, at] = (ga[rows, at] * slope).astype(BF16)
+            gp[rows, at] = (ga[rows, at].astype(F32) * slope).astype(BF16)
             return 0
 
         lax.fori_loop(0, tiles, tile, 0, unroll=UH)
@@ -313,37 +317,43 @@
             pair_done(0)
     p0(1).start()
 
-    grads = (zero, zero)
-    for ch in range(chunks):
-
-        def back(n, _, ch=ch):
+    wide = lax.broadcasted_iota(jnp.int32, (16, 256), 0) == lax.broadcasted_iota(jnp.int32, (16, 256), 1) // LANES
+    both_ones = jnp.where(wide, 1.0, 0.0).astype(BF16)
+
+    def back(ch):
+        for n in range(tiles):
             at = pl.ds(pl.multiple_of(ch * span + n * 256, 256), 256)
             gm = jnp.dot(w1t[...], gp[:, at], preferred_element_type=F32)
             for i in range(2):
                 gm_n[ch, pl.ds(n * 2 + i, patches, stride=NB), :] = gm[:, i * LANES : (i + 1) * LANES]
-            return 0
-
-        lax.fori_loop(0, tiles, back, 0, unroll=UB)
-
-        def sums(p, at, carry, ch=ch):
-            f, s, dg, ds = carry
-            rows = pl.ds(pl.multiple_of(p * NB, NB), NB)
+
+    def row_sums(ch, grads):
+        def sums(g, n, carry):
+            dg, ds = carry
+            rows = pl.ds(pl.multiple_of(g * LANES, 64), n)
             gm = gm_n[ch, rows, :]
             normed = normed_n[ch, rows, :]
             both = gm * normed
-            hit = lane == at
-            f = jnp.where(hit, jnp.sum(gm * gain, axis=-1, keepdims=True), f)
-            s = jnp.where(hit, jnp.sum(both * gain, axis=-1, keepdims=True), s)
-            return f, s, dg + both, ds + gm
-
-        for t, (f, s, dg, ds) in enumerate(lane_tiles(sums, (zero, zero, zero, zero))):
-            b_send[ch, :, pl.ds(t * LANES, LANES)] = f
-            b_send[ch, :, pl.ds((2 + t) * LANES, LANES)] = s
-            grads = (grads[0] + dg, grads[1] + ds)
+            gn = gm * gain
+            gm_n[ch, rows, :] = gn * inv_n[ch, rows, :]
+            pair = jnp.concatenate([gn.astype(BF16), (both * gain).astype(BF16)], axis=1)
+            total = contract_lanes(both_ones, pair)
+            b_send[ch, pl.ds(g, 1), :n] = total[0:1]
+            b_send[ch, pl.ds(second_row + g, 1), :n] = total[1:2]
+            return dg + both.reshape(-1, 8, LANES).sum(axis=0), ds + gm.reshape(-1, 8, LANES).sum(axis=0)
+
+        grads = over_blocks(sums, grads, unroll=UR)
         for j in range(1, n_chan):
             remote(b_send.at[ch], b_recv.at[ch, j], bs_sem.at[ch, j], br_sem.at[ch, j], me_d, chan_peer(j)).start()
-        if ch == 0:
-            pair_done(1)
+        return grads
+
+    grads = (jnp.zeros((8, LANES), F32),) * 2
+    back(0)
+    pair_done(1)
+    for ch in range(chunks):
+        if ch:
+            back(ch)
+        grads = row_sums(ch, grads)
 
     mine = jnp.concatenate([jnp.sum(v, axis=0, keepdims=True) for v in grads], axis=0)
     d_send[...] = mine
@@ -353,35 +363,22 @@
     group_done(0)
 
     for ch in range(chunks):
-        total = b_send[ch]
-        for j in range(1, n_chan):
-            remote(b_send.at[ch], b_recv.at[ch, j], bs_sem.at[ch, j], br_sem.at[ch, j], me_d, chan_peer(j)).wait_recv()
-            total = total + b_recv[ch, j]
-        inv = inv_d[ch]
-        f = total[:, : 2 * LANES] * inv / width
-        s = total[:, 2 * LANES :] * inv / width
-
-        for t in range(2):
-            lo = t * LANES
-            count = min(LANES, patches - lo)
-            cut = slice(lo, lo + LANES)
-
-            unroll = 32 if count == LANES else 34
-
-            def finish(q, carry, ch=ch, lo=lo, unroll=unroll):
-                i_t, f_t, s_t = carry
-                for i in range(unroll):
-                    p = lo + q * unroll + i
-                    rows = pl.ds(pl.multiple_of(p * NB, NB), NB)
-                    bs = pl.ds(ch * NB, NB)
-                    gn = gm_n[ch, rows, :] * gain
-                    v = u_v[p, bs, :].astype(F32) + column(i_t, i) * gn - column(f_t, i) - column(s_t, i) * normed_n[ch, rows, :]
-                    out_ref[p, bs, :] = v.astype(BF16)
-                return tuple(pltpu.roll(c, LANES - unroll, 1) for c in carry)
-
-            lax.fori_loop(0, count // unroll, finish, (inv[:, cut], f[:, cut], s[:, cut]))
-
-    group_done(1)
+        if ch == chunks - 1:
+            group_done(1)
+        totals = received(b_send, b_recv, bs_sem, br_sem, ch)
+        for dst, total in zip((first_d, second_d), totals):
+            dst[...] = total * inv_d[ch] / width
+
+        def finish(g, n, carry, ch=ch):
+            rows = pl.ds(pl.multiple_of(g * LANES, 64), n)
+            f = spread(first_d[pl.ds(g, 1), :])[:n]
+            q = spread(second_d[pl.ds(g, 1), :])[:n]
+            v = images_of(u_v, g, n, ch).astype(F32) + gm_n[ch, rows, :] - f - q * normed_n[ch, rows, :]
+            out_ref[pl.ds(g * 8, n // NB), pl.ds(ch * NB, NB), :] = v.astype(BF16).reshape(n // NB, NB, LANES)
+            return carry
+
+        over_blocks(finish, 0, unroll=UF)
+
     all_done(0)
     for j in range(1, n_dp):
         d = dp_peer(j)
@@ -415,7 +412,9 @@
     width = float(local * n_chan)
     scale = 1.0 / (images * n_dp)
     rows = hid // (groups * 4)
-    stat = (chunks, NB, 4 * LANES)
+    blocks = -(-patches // 8)
+    stat_rows = -(-blocks // 8) * 8 + blocks
+    stat = (chunks, stat_rows, LANES)
     vmem = pl.BlockSpec(memory_space=pltpu.VMEM)
     hbm = pl.BlockSpec(memory_space=pltpu.HBM)
     dma = pltpu.SemaphoreType.DMA
@@ -429,9 +428,14 @@
             jax.ShapeDtypeStruct((1, local), F32),
             jax.ShapeDtypeStruct((1, local), F32),
         ),
-        in_specs=[hbm, hbm] + [vmem] * 5,
+        in_specs=[hbm] * 7,
         out_specs=(vmem,) * 6,
         scratch_shapes=[
+            pltpu.VMEM((1, local), F32),
+            pltpu.VMEM((1, local), F32),
+            pltpu.VMEM((patches, hid), BF16),
+            pltpu.VMEM((1, hid), F32),
+            pltpu.VMEM((patches, hid), BF16),
             pltpu.VMEM((PP, hid), BF16),
             pltpu.VMEM((PP, hid), BF16),
             pltpu.VMEM((16, hid), F32),
@@ -442,18 +446,22 @@
             pltpu.VMEM((patches, images, local), BF16),
             pltpu.VMEM((PP, images * local), BF16),
             pltpu.VMEM((PP, images * local), BF16),
-            pltpu.VMEM((hid, images * local), F32),
+            pltpu.VMEM((hid, images * local), BF16),
             pltpu.VMEM((hid, images * local), BF16),
             pltpu.VMEM((hid // 2, NB * local), BF16),
             pltpu.VMEM((chunks, patches * NB, local), F32),
             pltpu.VMEM((chunks, patches * NB, local), F32),
+            pltpu.VMEM((chunks, patches * NB, local), F32),
             pltpu.VMEM((16 * NB, local), F32),
-            pltpu.VMEM((chunks, NB, 2 * LANES), F32),
+            pltpu.VMEM((chunks, blocks, LANES), F32),
+            pltpu.VMEM((chunks, blocks, LANES), F32),
+            pltpu.VMEM((blocks, LANES), F32),
+            pltpu.VMEM((blocks, LANES), F32),
             pltpu.VMEM((2, groups, 2, rows, 4 * LANES), F32),
             pltpu.VMEM(stat, F32),
-            pltpu.VMEM((chunks, n_chan, NB, 4 * LANES), F32),
+            pltpu.VMEM((chunks, n_chan, stat_rows, LANES), F32),
             pltpu.VMEM(stat, F32),
-            pltpu.VMEM((chunks, n_chan, NB, 4 * LANES), F32),
+            pltpu.VMEM((chunks, n_chan, stat_rows, LANES), F32),
             pltpu.VMEM((2, groups, rows, 4 * LANES), F32),
             pltpu.VMEM((2, groups, rows, 4 * LANES), F32),
             pltpu.VMEM((2, groups, rows, 4 * LANES), F32),
@@ -462,6 +470,7 @@
             pltpu.VMEM((2, local), F32),
             pltpu.VMEM((n_dp, 2, local), F32),
             dma((2, 3)),
+            dma((5,)),
             dma((chunks, n_chan)),
             dma((chunks, n_chan)),
             dma((chunks, n_chan)),

time: 75.2 us -> 66.5 us (0.88)
  Pallas kernels: 66.4 us -> 57.3 us
    pallas_call x1, Pallas kernels: 66.4 us -> 57.3 us  [per_device(): pl.pallas_call(functools.partial(kernel, n_dp, n_chan, patches, width, sc...]
where the time goes in v3:
time: 66.5 us; the launch traced here: 65.9 us
  Pallas kernels  57.3 us (86%)
  local copies, waits for them, and re-layouts  8.01 us (12%)
    pallas_call x1, Pallas kernels, per_device(): pl.pallas_call(functools.partial(kernel, n_dp, n_chan, patches, width, sc...  57.3 us
    unnamed x16, local copies, waits for them, and re-layouts  8.01 us

profile of v3, /device:TPU:2, one launch (start us, length us, event | category | flops | bytes accessed | tf_op | source)
XLA Modules:
  0.0 65.9 jit_solution(6987237459806762119)
XLA Ops:
  0.6 0.0 copy-start
  0.6 0.9 %copy-done = bf16[512,196]{0,1:T(8,128)(2,1)S(1)} copy-done((bf16[512,196]{0,1:T(8,128)(2,1)S(1)}, bf16[512,196]{0,1:T(8,128)(2,1)}, u32[]{:S(2)}) %copy-start) | copy-done | bytes 200728
  1.6 0.0 copy-start.1
  1.6 0.9 %copy-done.1 = bf16[196,512]{1,0:T(8,128)(2,1)S(1)} copy-done((bf16[196,512]{1,0:T(8,128)(2,1)S(1)}, bf16[196,512]{1,0:T(8,128)(2,1)}, u32[]{:S(2)}) %copy-start.1) | copy-done | bytes 200728
  2.5 0.0 copy-start.2
  2.5 0.7 %copy-done.2 = f32[512]{0:T(512)S(1)} copy-done((f32[512]{0:T(512)S(1)}, f32[512]{0:T(512)}, u32[]{:S(2)}) %copy-start.2) | copy-done | bytes 2072
  3.2 0.0 copy-start.3
  3.2 0.7 copy-done.3
  3.8 0.0 copy-start.4
  3.8 0.7 copy-done.4
  4.5 57.3 %shard_map.118 = (bf16[196,48,128]{2,1,0:T(8,128)(2,1)S(1)}, f32[16,196]{1,0:T(8,128)S(1)}, f32[16,196]{1,0:T(8,128)S(1)}, f32[1,16]{1,0:T(1,128)S(1)}, f32[1,128]{1,0:T(1,128)S(1)}, /*index=5*/f32[1,128]{1,0:T(1,128)S(1)}) custom-call(bf16[196,48,128]{2,1,0:T(8,128)(2,1)} %bitcast.20, bf16[196,48,128]{2,1,0:T(8,128)(2,1)} %bitcast.21, ...), custom_call_target="tpu_custom_call" | custom-call | tf_op jit(solution)/shard_map/pallas_call | solution.py:421
  61.8 1.4 %copy.19 = bf16[48,196,128]{2,0,1:T(8,128)(2,1)} copy(bf16[48,196,128]{2,0,1:T(8,128)(2,1)S(1)} %bitcast.11) | data formatting | bytes 4816896
  63.2 0.6 copy.20
  63.8 0.6 copy.21
  64.4 0.5 copy.22
  64.9 0.5 copy.23
  65.4 0.5 copy.24
Async XLA Ops:
  0.6 0.9 %copy-start = (bf16[512,196]{0,1:T(8,128)(2,1)S(1)}, bf16[512,196]{0,1:T(8,128)(2,1)}, u32[]{:S(2)}) copy-start(bf16[512,196]{0,1:T(8,128)(2,1)} %param.10) | copy-start | bytes 602116
  1.6 0.9 %copy-start.1 = (bf16[196,512]{1,0:T(8,128)(2,1)S(1)}, bf16[196,512]{1,0:T(8,128)(2,1)}, u32[]{:S(2)}) copy-start(bf16[196,512]{1,0:T(8,128)(2,1)} %w2_hbm.1) | copy-start | bytes 602116
  2.5 0.7 %copy-start.2 = (f32[512]{0:T(512)S(1)}, f32[512]{0:T(512)}, u32[]{:S(2)}) copy-start(f32[512]{0:T(512)} %param.11) | copy-start | bytes 6148
  3.2 0.7 copy-start.3
  3.8 0.7 copy-start.4

commit v4 on v3

--- a/solution.py
+++ b/solution.py
@@ -306,17 +306,6 @@
         owned_b.append(jnp.sum(jnp.where(here, total[:, patches : patches + 1], 0.0), axis=0, keepdims=True))
         second_ref[pl.ds(h * 8, 8), :] = total[:, 256 : 256 + patches]
 
-    for ch in range(chunks):
-        normalise(ch)
-    for ch in range(chunks):
-        hidden(0, ch)
-    p0(0).start()
-    for ch in range(chunks):
-        hidden(1, ch)
-        if ch == 0:
-            pair_done(0)
-    p0(1).start()
-
     wide = lax.broadcasted_iota(jnp.int32, (16, 256), 0) == lax.broadcasted_iota(jnp.int32, (16, 256), 1) // LANES
     both_ones = jnp.where(wide, 1.0, 0.0).astype(BF16)
 
@@ -348,11 +337,23 @@
         return grads
 
     grads = (jnp.zeros((8, LANES), F32),) * 2
-    back(0)
-    pair_done(1)
-    for ch in range(chunks):
-        if ch:
-            back(ch)
+    for ch in range(chunks):
+        normalise(ch)
+    for ch in range(chunks):
+        hidden(0, ch)
+    p0(0).start()
+    for ch in range(chunks):
+        hidden(1, ch)
+        if ch == 0:
+            pair_done(0)
+            back(0)
+            grads = row_sums(0, grads)
+    p0(1).start()
+
+    for ch in range(1, chunks):
+        back(ch)
+        if ch == 1:
+            pair_done(1)
         grads = row_sums(ch, grads)
 
     mine = jnp.concatenate([jnp.sum(v, axis=0, keepdims=True) for v in grads], axis=0)
@@ -360,9 +361,10 @@
     d_recv[me_d] = mine
     for j in range(1, n_dp):
         remote(d_send, d_recv.at[me_d], ds_sem.at[j], dr_sem.at[me_d], dp_peer(j), me_c).start()
-    group_done(0)
-
-    for ch in range(chunks):
+
+    for ch in range(chunks):
+        if ch == 1:
+            group_done(0)
         if ch == chunks - 1:
             group_done(1)
         totals = received(b_send, b_recv, bs_sem, br_sem, ch)
@@ -488,13 +490,13 @@
             collective_id=0, has_side_effects=True, vmem_limit_bytes=VMEM_LIMIT
         ),
     )(
-        inputs.transpose(1, 0, 2),
-        upstream.transpose(1, 0, 2),
-        norm_gain.reshape(1, local),
-        norm_bias.reshape(1, local),
-        w_first.T,
-        b_first.reshape(1, hid),
-        w_second,
+        pltpu.with_memory_space_constraint(inputs.transpose(1, 0, 2), pltpu.HBM),
+        pltpu.with_memory_space_constraint(upstream.transpose(1, 0, 2), pltpu.HBM),
+        pltpu.with_memory_space_constraint(norm_gain.reshape(1, local), pltpu.HBM),
+        pltpu.with_memory_space_constraint(norm_bias.reshape(1, local), pltpu.HBM),
+        pltpu.with_memory_space_constraint(w_first.T, pltpu.HBM),
+        pltpu.with_memory_space_constraint(b_first.reshape(1, hid), pltpu.HBM),
+        pltpu.with_memory_space_constraint(w_second, pltpu.HBM),
     )
     return (
         out.transpose(1, 0, 2),

time: 66.5 us -> 61.7 us (0.928)
  local copies, waits for them, and re-layouts: 8.01 us -> 4.17 us
  Pallas kernels: 57.3 us -> 56.6 us
    unnamed x16 -> x6, local copies, waits for them, and re-layouts: 8.01 us -> 4.17 us
where the time goes in v4:
time: 61.7 us; the launch traced here: 61.4 us
  Pallas kernels  56.6 us (92%)
  local copies, waits for them, and re-layouts  4.17 us (7%)
  between operations  0.65 us (1%)
    pallas_call x1, Pallas kernels, per_device(): pl.pallas_call(functools.partial(kernel, n_dp, n_chan, patches, width, sc...  56.6 us
    unnamed x6, local copies, waits for them, and re-layouts  4.17 us

profile of v4, /device:TPU:2, one launch (start us, length us, event | category | flops | bytes accessed | tf_op | source)
XLA Modules:
  0.0 61.4 jit_solution(12997336198384929465)
XLA Ops:
  0.6 56.6 %shard_map.118 = (bf16[196,48,128]{2,1,0:T(8,128)(2,1)S(1)}, f32[16,196]{1,0:T(8,128)S(1)}, f32[16,196]{1,0:T(8,128)S(1)}, f32[1,16]{1,0:T(1,128)S(1)}, f32[1,128]{1,0:T(1,128)S(1)}, /*index=5*/f32[1,128]{1,0:T(1,128)S(1)}) custom-call(bf16[196,48,128]{2,1,0:T(8,128)(2,1)} %bitcast.16, bf16[196,48,128]{2,1,0:T(8,128)(2,1)} %bitcast.17, f32[1,128]{1,0:T(1,128)} %bitcast.20, ...), custom_call_target="tpu_custom_call" | custom-call | tf_op jit(solution)/shard_map/pallas_call | solution.py:423
  57.3 1.4 %copy.19 = bf16[48,196,128]{2,0,1:T(8,128)(2,1)} copy(bf16[48,196,128]{2,0,1:T(8,128)(2,1)S(1)} %bitcast.11) | data formatting | bytes 4816896
  58.7 0.6 copy.20
  59.3 0.6 copy.21
  59.9 0.5 copy.22
  60.4 0.5 copy.23
  60.9 0.5 copy.24

commit v5 on v4

--- a/solution.py
+++ b/solution.py
@@ -29,7 +29,7 @@
 def kernel(
     n_dp, n_chan, patches, width, scale,
     x_hbm, u_hbm, gain_hbm, bias_hbm, w1_hbm, bf_hbm, w2_hbm,
-    out_ref, first_ref, second_ref, first_b_ref, gain_g_ref, shift_g_ref,
+    out_ref, owned_ref, vec_ref,
     gain_ref, bias_ref, w1_ref, bf_ref, w2_ref, w1f, w2f, wtail, w1a, w1t, w2t,
     x_v, u_v, mx, up, ga, gp, act, normed_n, inv_n, gm_n, tmp, mean_d, inv_d, first_d, second_d, acc,
     a_send, a_recv, b_send, b_recv, p0_recv, csum, c1_recv, c1_sum, c2_recv, d_send, d_recv,
@@ -58,6 +58,11 @@
             device_id={"dp": dp, "chan": chan}, device_id_type=pl.DeviceIdType.MESH,
         )
 
+    far_groups = sorted(range(1, groups), key=lambda j: -min(j, groups - j))
+    far_dp = sorted(range(1, n_dp), key=lambda j: -min(j, n_dp - j))
+    turn = n_chan // 2
+    far_chan = sorted(range(1, n_chan), key=lambda j: (-min(j % turn, turn - j % turn), -j))
+
     barrier = pltpu.get_barrier_semaphore()
     for j in range(1, n_chan):
         pl.semaphore_signal(barrier, inc=1, device_id={"dp": me_d, "chan": chan_peer(j)}, device_id_type=pl.DeviceIdType.MESH)
@@ -83,7 +88,7 @@
         load(1, u_hbm, u_v, part).start()
 
     blocks = -(-patches // 8)
-    second_row = -(-blocks // 8) * 8
+    second_row = blocks
     eye = lax.broadcasted_iota(jnp.int32, (LANES, LANES), 0) == lax.broadcasted_iota(jnp.int32, (LANES, LANES), 1)
 
     def dense(value):
@@ -129,7 +134,7 @@
         over_blocks(stat, 0, part * 8, part * 8 + 8 if part < 2 else None, US)
     pl.semaphore_wait(barrier, n_chan - 1 + n_dp - 1)
     for ch in range(chunks):
-        for j in range(1, n_chan):
+        for j in far_chan:
             remote(a_send.at[ch], a_recv.at[ch, j], as_sem.at[ch, j], ar_sem.at[ch, j], me_d, chan_peer(j)).start()
 
     def select(lo, count):
@@ -244,7 +249,7 @@
             t = pre * 0.7071067811865476
             cdf = 0.5 * lax.erf(t) + 0.5
             act[:, pl.ds(pl.multiple_of(n * 256, 256), 256)] = (pre * cdf).astype(BF16)
-            slope = cdf + (t * 0.5641895835477563) * jnp.exp(-(t * t))
+            slope = cdf + (t * 0.5641895835477563) * jnp.exp2((t * t) * -1.4426950408889634)
             gp[rows, at] = (ga[rows, at].astype(F32) * slope).astype(BF16)
             return 0
 
@@ -279,7 +284,7 @@
     def pair_done(h):
         p0(h).wait()
         csum[h] = acc[h, :, core] + p0_recv[h]
-        for j in range(1, groups):
+        for j in far_groups:
             c1(h, j).start()
 
     def group_done(h):
@@ -291,7 +296,7 @@
             total = total + c1_recv[h, g]
         c1_sum[h] = total
         c2_recv[h, me_c] = total
-        for j in range(1, n_chan):
+        for j in far_chan:
             c2(h, j).start()
 
     def all_done(h):
@@ -301,10 +306,10 @@
         for c in range(1, n_chan):
             total = total + c2_recv[h, c]
         total = total * scale
-        first_ref[pl.ds(h * 8, 8), :] = total[:, :patches]
+        owned_ref[0, pl.ds(h * 8, 8), :] = total[:, :patches]
         here = lax.broadcasted_iota(jnp.int32, (8, LANES), 0) + h * 8 == lax.broadcasted_iota(jnp.int32, (8, LANES), 1)
         owned_b.append(jnp.sum(jnp.where(here, total[:, patches : patches + 1], 0.0), axis=0, keepdims=True))
-        second_ref[pl.ds(h * 8, 8), :] = total[:, 256 : 256 + patches]
+        owned_ref[1, pl.ds(h * 8, 8), :] = total[:, 256 : 256 + patches]
 
     wide = lax.broadcasted_iota(jnp.int32, (16, 256), 0) == lax.broadcasted_iota(jnp.int32, (16, 256), 1) // LANES
     both_ones = jnp.where(wide, 1.0, 0.0).astype(BF16)
@@ -332,7 +337,7 @@
             return dg + both.reshape(-1, 8, LANES).sum(axis=0), ds + gm.reshape(-1, 8, LANES).sum(axis=0)
 
         grads = over_blocks(sums, grads, unroll=UR)
-        for j in range(1, n_chan):
+        for j in far_chan:
             remote(b_send.at[ch], b_recv.at[ch, j], bs_sem.at[ch, j], br_sem.at[ch, j], me_d, chan_peer(j)).start()
         return grads
 
@@ -359,7 +364,7 @@
     mine = jnp.concatenate([jnp.sum(v, axis=0, keepdims=True) for v in grads], axis=0)
     d_send[...] = mine
     d_recv[me_d] = mine
-    for j in range(1, n_dp):
+    for j in far_dp:
         remote(d_send, d_recv.at[me_d], ds_sem.at[j], dr_sem.at[me_d], dp_peer(j), me_c).start()
 
     for ch in range(chunks):
@@ -388,10 +393,9 @@
     vec = d_recv[0]
     for d in range(1, n_dp):
         vec = vec + d_recv[d]
-    gain_g_ref[...] = vec[0:1] * scale
-    shift_g_ref[...] = vec[1:2] * scale
+    vec_ref[pl.ds(0, 2), :] = vec * scale
     all_done(1)
-    first_b_ref[...] = (owned_b[0] + owned_b[1])[:, :16]
+    vec_ref[pl.ds(2, 1), :] = owned_b[0] + owned_b[1]
 
     for ch in range(chunks):
         for j in range(1, n_chan):
@@ -415,23 +419,20 @@
     scale = 1.0 / (images * n_dp)
     rows = hid // (groups * 4)
     blocks = -(-patches // 8)
-    stat_rows = -(-blocks // 8) * 8 + blocks
+    stat_rows = 2 * blocks
     stat = (chunks, stat_rows, LANES)
     vmem = pl.BlockSpec(memory_space=pltpu.VMEM)
     hbm = pl.BlockSpec(memory_space=pltpu.HBM)
     dma = pltpu.SemaphoreType.DMA
-    out, first, second, first_b, gain_g, shift_g = pl.pallas_call(
+    out, owned, vec = pl.pallas_call(
         functools.partial(kernel, n_dp, n_chan, patches, width, scale),
         out_shape=(
             jax.ShapeDtypeStruct((patches, images, local), BF16),
-            jax.ShapeDtypeStruct((2 * rows, patches), F32),
-            jax.ShapeDtypeStruct((2 * rows, patches), F32),
-            jax.ShapeDtypeStruct((1, 2 * rows), F32),
-            jax.ShapeDtypeStruct((1, local), F32),
-            jax.ShapeDtypeStruct((1, local), F32),
+            jax.ShapeDtypeStruct((2, 2 * rows, patches), F32),
+            jax.ShapeDtypeStruct((3, local), F32),
         ),
         in_specs=[hbm] * 7,
-        out_specs=(vmem,) * 6,
+        out_specs=(vmem,) * 3,
         scratch_shapes=[
             pltpu.VMEM((1, local), F32),
             pltpu.VMEM((1, local), F32),
@@ -500,11 +501,11 @@
     )
     return (
         out.transpose(1, 0, 2),
-        first,
-        second.T,
-        first_b[0],
-        gain_g[0],
-        shift_g[0],
+        owned[0],
+        owned[1].T,
+        vec[2, : 2 * rows],
+        vec[0],
+        vec[1],
     )
 
 

time: 61.7 us -> 59.3 us (0.961)
  Pallas kernels: 56.6 us -> 55.5 us
  local copies, waits for them, and re-layouts: 4.17 us -> 3.07 us
    unnamed x6 -> x1, local copies, waits for them, and re-layouts: 4.17 us -> 1.42 us
    pallas_call x1, Pallas kernels: 56.6 us -> 55.5 us  [per_device(): pl.pallas_call(functools.partial(kernel, n_dp, n_chan, patches, width, sc...]
    squeeze x0 -> x2, local copies, waits for them, and re-layouts: none -> 1.03 us  [the longest x1 0.52 us: per_device(): vec[1]]
where the time goes in v5:
time: 59.3 us; the launch traced here: 59.2 us
  Pallas kernels  55.5 us (94%)
  local copies, waits for them, and re-layouts  3.07 us (5%)
  between operations  0.64 us (1%)
    pallas_call x1, Pallas kernels, per_device(): pl.pallas_call(functools.partial(kernel, n_dp, n_chan, patches, width, sc...  55.5 us
    unnamed x1, local copies, waits for them, and re-layouts  1.42 us

profile of v5, /device:TPU:2, one launch (start us, length us, event | category | flops | bytes accessed | tf_op | source)
XLA Modules:
  0.0 59.2 jit_solution(7536737737448521789)
XLA Ops:
  0.6 55.5 %shard_map.118 = (bf16[196,48,128]{2,1,0:T(8,128)(2,1)S(1)}, f32[2,16,196]{2,1,0:T(8,128)S(1)}, f32[3,128]{1,0:T(4,128)S(1)}) custom-call(bf16[196,48,128]{2,1,0:T(8,128)(2,1)} %bitcast.20, bf16[196,48,128]{2,1,0:T(8,128)(2,1)} %bitcast.21, f32[1,128]{1,0:T(1,128)} %bitcast.24, f32[1,128]{1,0:T(1,128)} %bitcast.25, bf16[196,512]{1,0:T(8,128)(2,1)} %bitcast.22, ...), custom_call_target="tpu_custom_call" | custom-call | tf_op jit(solution)/shard_map/pallas_call | solution.py:427
  56.1 0.5 slice_bitcast_fusion.2
  56.7 0.6 %slice_bitcast_fusion = (f32[196,16]{0,1:T(8,128)}, f32[16,196]{1,0:T(8,128)}) fusion(f32[2,16,196]{2,1,0:T(8,128)S(1)} %get-tuple-element.10), kind=kLoop, calls=%fused_computation | loop fusion | bytes 50176 | tf_op jit(solution)/shard_map/transpose | solution.py:505
  57.3 0.5 slice_bitcast_fusion.4
  57.8 1.4 %copy.14 = bf16[48,196,128]{2,0,1:T(8,128)(2,1)} copy(bf16[48,196,128]{2,0,1:T(8,128)(2,1)S(1)} %bitcast.19) | data formatting | bytes 4816896

commit v6 on v5

--- a/solution.py
+++ b/solution.py
@@ -352,13 +352,12 @@
         if ch == 0:
             pair_done(0)
             back(0)
-            grads = row_sums(0, grads)
     p0(1).start()
+    grads = row_sums(0, grads)
+    pair_done(1)
 
     for ch in range(1, chunks):
         back(ch)
-        if ch == 1:
-            pair_done(1)
         grads = row_sums(ch, grads)
 
     mine = jnp.concatenate([jnp.sum(v, axis=0, keepdims=True) for v in grads], axis=0)

time: 59.3 us -> 59.5 us (level)
  no operation moved by 1% of the time
where the time goes in v6:
time: 59.5 us; the launch traced here: 59.1 us
  Pallas kernels  55.4 us (93%)
  local copies, waits for them, and re-layouts  3.07 us (5%)
  between operations  0.64 us (1%)
    pallas_call x1, Pallas kernels, per_device(): pl.pallas_call(functools.partial(kernel, n_dp, n_chan, patches, width, sc...  55.4 us
    unnamed x1, local copies, waits for them, and re-layouts  1.42 us

profile of v6, /device:TPU:2, one launch (start us, length us, event | category | flops | bytes accessed | tf_op | source)
XLA Modules:
  0.0 59.1 jit_solution(3701623527188150235)
XLA Ops:
  0.6 55.4 %shard_map.118 = (bf16[196,48,128]{2,1,0:T(8,128)(2,1)S(1)}, f32[2,16,196]{2,1,0:T(8,128)S(1)}, f32[3,128]{1,0:T(4,128)S(1)}) custom-call(bf16[196,48,128]{2,1,0:T(8,128)(2,1)} %bitcast.20, bf16[196,48,128]{2,1,0:T(8,128)(2,1)} %bitcast.21, f32[1,128]{1,0:T(1,128)} %bitcast.24, f32[1,128]{1,0:T(1,128)} %bitcast.25, bf16[196,512]{1,0:T(8,128)(2,1)} %bitcast.22, ...), custom_call_target="tpu_custom_call" | custom-call | tf_op jit(solution)/shard_map/pallas_call | solution.py:426
  56.1 0.5 slice_bitcast_fusion.2
  56.6 0.6 %slice_bitcast_fusion = (f32[196,16]{0,1:T(8,128)}, f32[16,196]{1,0:T(8,128)}) fusion(f32[2,16,196]{2,1,0:T(8,128)S(1)} %get-tuple-element.10), kind=kLoop, calls=%fused_computation | loop fusion | bytes 50176 | tf_op jit(solution)/shard_map/transpose | solution.py:504
  57.2 0.5 slice_bitcast_fusion.4
  57.7 1.4 %copy.14 = bf16[48,196,128]{2,0,1:T(8,128)(2,1)} copy(bf16[48,196,128]{2,0,1:T(8,128)(2,1)S(1)} %bitcast.19) | data formatting | bytes 4816896
